TPU v7x, 128 devices: a whole 4x4x4 slice. The times are simulated.
128 devices in a mesh: row: 8 (over z, x_lo), col: 16 (over y, x_hi, core).
Axes of the slice: x: 4 (x_hi: 2, x_lo: 2; x = x_hi * 2 + x_lo), y: 4, z: 4, core: 2. Of those that a mesh axis runs over, the one named last changes fastest.
Arguments:
- cell_index: int32 [2, 3, 262144], P(None, None, ('row', 'col')), may hold values from 0 to 255, as said below
- fraction: float32 [2, 3, 262144], P(None, None, ('row', 'col')), may hold values from 0 to 1
- charge: float32 [2, 262144], P(None, ('row', 'col')), may hold values from -4 to 4
- atom_count: int32 [2, 128], P(None, ('row', 'col')), may hold values from 1024 to 2048, as said below
- influence: float32 [256, 256, 256], P('row', 'col'), as said below
Outputs:
- forces: float32 [2, 3, 262144], P(None, None, ('row', 'col'))
Inputs may be any that keep to these rules, and one draw needn't show every extreme that they name: `cell_index`: slot a belongs to pencil p = a // 2048; with P = 16, its first cell index lies in [(p // P) * 32, (p // P + 1) * 32) and its second in [(p % P) * 16, (p % P + 1) * 16). `atom_count`: in every frame some pencil has all 2048 slots live. Even: influence[a, b, c] equals influence[(-a) mod 256, (-b) mod 256, (-c) mod 256]; it is 0 at the root and positive elsewhere.
All inputs are finite; a program needn't handle non-finite values.
Results may differ from a plain program's by a relative error of at most 0.0003.
Values sent between devices are 32-bit elements; how exact they have to be, the bound alone decides.
A program may use at most 128 MiB of HBM per device.

v0:
```python
import functools

import jax
import jax.numpy as jnp
import numpy as np
from jax import lax
from jax.experimental import pallas as pl
from jax.experimental.pallas import tpu as pltpu
from jax.sharding import PartitionSpec as P

F32 = jnp.float32
BF16 = jnp.bfloat16
MESH = pl.DeviceIdType.MESH

K = 256
ROWS = 8
COLS = 16
DEVS = ROWS * COLS
ATOMS = 2048
CHUNK = 512
CHUNKS = ATOMS // CHUNK
GCHUNK = 256
GCHUNKS = ATOMS // GCHUNK

YH, XH, CH = 160, 80, 48
HALO = YH + XH + CH


def halves(x):
    top = x.astype(BF16)
    return top, (x - top.astype(F32)).astype(BF16)


def np_halves(x):
    x = np.asarray(x, np.float32)
    top = x.astype(jnp.bfloat16)
    return [top, (x - top.astype(np.float32)).astype(jnp.bfloat16)]


def tables():
    d = np.arange(DEVS)
    waves = np.concatenate([16 * (d % COLS) + 2 * (d // COLS) + p for p in range(2)])
    turn = 2.0 * np.pi / K
    angle = (waves[:, None] * np.arange(K)[None, :] % K) * turn
    out = np_halves(np.cos(angle)) + np_halves(np.sin(angle))
    k1 = np.arange(256)
    k1x, k1y = k1 // 16, k1 % 16
    src = np.arange(256)
    xh, rc = src // DEVS, src % DEVS
    rx, cc = 2 * (rc // COLS) + xh, rc % COLS
    angle = ((k1x[:, None] * rx[None, :] + k1y[:, None] * cc[None, :]) % 16) * (16 * turn)
    out += np_halves(np.cos(angle)) + np_halves(np.sin(angle))
    out += np_halves(np.cos(angle.T)) + np_halves(np.sin(angle.T))
    spot = np.arange(256)
    xl, yl = spot // 16, spot % 16
    k2 = np.arange(256)
    k2y, k2x = k2 // 16, k2 % 16
    angle = ((xl[:, None] * k2x[None, :] + yl[:, None] * k2y[None, :]) % 16) * (16 * turn)
    out += np_halves(np.cos(angle)) + np_halves(np.sin(angle))
    angle = ((k1x[:, None] * xl[None, :] + k1y[:, None] * yl[None, :]) % K) * turn
    out += [np.cos(angle).astype(np.float32), np.sin(angle).astype(np.float32)]
    return out


def spline_values(f):
    nothing = jnp.zeros_like(f)
    levels = [f, 1.0 - f]
    slopes = levels
    for degree in range(3, 7):
        padded = levels + [nothing]
        following = []
        for o in range(degree):
            value = (f + float(o)) * padded[o]
            if o > 0:
                value = value + (float(degree - o) - f) * padded[o - 1]
            following.append(value * (1.0 / (degree - 1)))
        if degree == 6:
            slopes = [padded[0]] + [padded[o] - padded[o - 1] for o in range(1, 6)]
        levels = following
    return levels, slopes


def dot_nn(a, b):
    return lax.dot_general(a, b, (((1,), (0,)), ((), ())), preferred_element_type=F32)


def dot_nt(a, b):
    return lax.dot_general(a, b, (((1,), (1,)), ((), ())), preferred_element_type=F32)


def triple(dot, a, b):
    return dot(a[0], b[0]) + dot(a[0], b[1]) + dot(a[1], b[0])


def dense(gap, rows):
    total = jnp.where(gap == 0, rows[0], 0.0)
    for j in range(1, 6):
        total = jnp.where(gap == j, rows[j], total)
    return total


def kernel(
    cell, frac, charge, count, infl,
    zc0, zc1, zs0, zs1, fc0, fc1, fs0, fs1, gc0, gc1, gs0, gs1, lc0, lc1, ls0, ls1, twc, tws,
    forces,
    w_scr, x_scr, y_scr, yq_scr, z_hi, z_lo, sx_scr, sy_scr, sz_hi, sz_lo,
    p_hi, p_lo, hal, yr, xr, cr, mesh, gsend, grecv, green,
    sbuf, rbuf, tbuf, qbuf, pot, ys, yb, xb, cb, fint, fhal,
    sems,
):
    row = lax.axis_index("row")
    col = lax.axis_index("col")
    me = row * COLS + col
    up_r, dn_r = lax.rem(row + 1, ROWS), lax.rem(row + ROWS - 1, ROWS)
    up_c, dn_c = lax.rem(col + 1, COLS), lax.rem(col + COLS - 1, COLS)

    barrier = pltpu.get_barrier_semaphore()

    def greet(k, carry):
        dr = lax.rem(row + k // COLS, ROWS)
        dc = lax.rem(col + lax.rem(k, COLS), COLS)
        pl.semaphore_signal(barrier, inc=1, device_id=(dr, dc), device_id_type=MESH)
        return carry

    lax.fori_loop(1, DEVS, greet, 0)

    for k in range(16):
        gsend[k // 2, k % 2] = infl[:, k, :]

    slot = lax.broadcasted_iota(jnp.int32, (1, ATOMS), 1)
    for s in range(2):
        values, slopes = spline_values(frac[s])
        for j in range(6):
            w_scr[s, 0, j] = values[j]
            w_scr[s, 1, j] = slopes[j]
        yq_scr[s, 24:25] = jnp.where(slot < count[s : s + 1, 0:1], charge[s : s + 1], 0.0)

    def spans(i):
        s = i // CHUNKS
        return s, pl.ds(pl.multiple_of(lax.rem(i, CHUNKS) * CHUNK, CHUNK), CHUNK)

    def positions(n, near):
        spot = lax.broadcasted_iota(jnp.int32, (n, CHUNK), 0)
        return jnp.where(spot < near, spot, spot - n)

    def rows_of(s, kind, dim, lanes):
        return [w_scr[s, kind, j, dim : dim + 1, lanes] for j in range(6)]

    def build(i, carry):
        s, lanes = spans(i)
        gap = (cell[s, 0:1, lanes] - row * 32) - positions(40, 32)
        x_scr[s, :, lanes] = dense(gap, rows_of(s, 0, 0, lanes))
        gap = (cell[s, 1:2, lanes] - col * 16) - positions(24, 16)
        y = dense(gap, rows_of(s, 0, 1, lanes))
        y_scr[s, :, lanes] = y
        yq_scr[s, 0:24, lanes] = y * yq_scr[s, 24:25, lanes]
        gap = (cell[s, 2:3, lanes] - positions(256, 256)) & 255
        top, rest = halves(dense(gap, rows_of(s, 0, 2, lanes)))
        z_hi[s, :, lanes] = top
        z_lo[s, :, lanes] = rest
        return carry

    def build_slopes(i, carry):
        s, lanes = spans(i)
        gap = (cell[s, 0:1, lanes] - row * 32) - positions(40, 32)
        sx_scr[s, :, lanes] = dense(gap, rows_of(s, 1, 0, lanes))
        gap = (cell[s, 1:2, lanes] - col * 16) - positions(24, 16)
        sy_scr[s, :, lanes] = dense(gap, rows_of(s, 1, 1, lanes))
        gap = (cell[s, 2:3, lanes] - positions(256, 256)) & 255
        top, rest = halves(dense(gap, rows_of(s, 1, 2, lanes)))
        sz_hi[s, :, lanes] = top
        sz_lo[s, :, lanes] = rest
        return carry

    lax.fori_loop(0, 2 * CHUNKS, build, 0)

    def put(at, value):
        top, rest = halves(value)
        p_hi[at : at + value.shape[0], :] = top
        p_lo[at : at + value.shape[0], :] = rest

    def accumulate(ref, s, lanes, n):
        a = p_hi[0:n, :], p_lo[0:n, :]
        b = z_hi[s, :, lanes], z_lo[s, :, lanes]
        ref[s] += triple(dot_nt, a, b)

    def halo_chunk(i, carry):
        s, lanes = spans(i)
        for k in range(5):
            put(32 * k, x_scr[s, 0:32, lanes] * yq_scr[s, 19 + k : 20 + k, lanes])
        for k in range(5):
            put(YH + 16 * k, yq_scr[s, 0:16, lanes] * x_scr[s, 35 + k : 36 + k, lanes])
        edge = yq_scr[s, 16:24, lanes]
        for k in range(3):
            first = edge * x_scr[s, 35 + 2 * k : 36 + 2 * k, lanes]
            if k < 2:
                second = edge * x_scr[s, 36 + 2 * k : 37 + 2 * k, lanes]
            else:
                second = jnp.zeros_like(first)
            put(YH + XH + 16 * k, jnp.concatenate([first, second], axis=0))
        accumulate(hal, s, lanes, HALO)
        return carry

    hal[...] = jnp.zeros_like(hal)
    lax.fori_loop(0, 2 * CHUNKS, halo_chunk, 0)

    pl.semaphore_wait(barrier, DEVS - 1)

    def remote(src, dst, pair, dr, dc):
        return pltpu.make_async_remote_copy(
            src_ref=src, dst_ref=dst, send_sem=sems.at[2 * pair], recv_sem=sems.at[2 * pair + 1],
            device_id=(dr, dc), device_id_type=MESH,
        )

    out_halo = [
        remote(hal.at[:, 0:YH], yr, 0, row, dn_c),
        remote(hal.at[:, YH : YH + XH], xr, 1, dn_r, col),
        remote(hal.at[:, YH + XH : HALO], cr, 2, dn_r, dn_c),
    ]
    for copy in out_halo:
        copy.start()

    def send_green(k, carry):
        there = lax.rem(row + k, ROWS)
        remote(gsend.at[there], grecv.at[row], 3, there, col).start()
        return carry

    lax.fori_loop(1, ROWS, send_green, 0)
    grecv[row] = gsend[row]

    def inner_chunk(i, carry):
        s, lanes = spans(i)
        for x in range(32):
            put(16 * x, yq_scr[s, 0:16, lanes] * x_scr[s, x : x + 1, lanes])
        accumulate(mesh, s, lanes, 512)
        return carry

    mesh[...] = jnp.zeros_like(mesh)
    lax.fori_loop(0, 2 * CHUNKS, inner_chunk, 0)

    for copy in out_halo:
        copy.wait()
    for s in range(2):
        view = mesh.at[s].reshape(32, 16, 256)
        for k in range(5):
            view[:, 11 + k, :] += yr[s, 32 * k : 32 * k + 32]
        for k in range(5):
            view[27 + k] += xr[s, 16 * k : 16 * k + 16]
            view[27 + k, 8:16] += cr[s, 8 * k : 8 * k + 8]

    zc, zs = (zc0[...], zc1[...]), (zs0[...], zs1[...])
    for xh in range(2):
        lo = slice(256 * xh, 256 * xh + 256)
        m0, m1 = halves(mesh[0, lo, :]), halves(mesh[1, lo, :])
        re = triple(dot_nt, zc, m0) + triple(dot_nt, zs, m1)
        im = triple(dot_nt, zc, m1) - triple(dot_nt, zs, m0)
        for par in range(2):
            sbuf[:, 4 * par + xh, :] = re[128 * par : 128 * par + 128]
            sbuf[:, 4 * par + 2 + xh, :] = im[128 * par : 128 * par + 128]

    def exchange(src, dst, pair):
        def send(k, carry):
            dr = lax.rem(row + k // COLS, ROWS)
            dc = lax.rem(col + lax.rem(k, COLS), COLS)
            remote(src.at[dr * COLS + dc], dst.at[me], pair, dr, dc).start()
            return carry

        lax.fori_loop(1, DEVS, send, 0)
        dst[me] = src[me]
        return remote(src.at[0 : DEVS - 1], dst.at[0 : DEVS - 1], pair, up_r, col)

    forward = exchange(sbuf, rbuf, 4)

    remote(gsend.at[0 : ROWS - 1], grecv.at[0 : ROWS - 1], 3, up_r, col).wait()
    i0 = lax.broadcasted_iota(jnp.int32, (256, 256), 0)
    i1 = lax.broadcasted_iota(jnp.int32, (256, 256), 1)
    own = (i1 & 15) == (i0 >> 4)
    same = (i0 >> 4) == (i1 & 15)
    green[...] = jnp.zeros_like(green)

    def permute_green(k2y, carry):
        pick = jnp.where(same & ((i1 >> 4) == k2y), 1.0, 0.0).astype(BF16)
        for par in range(2):
            start = pl.multiple_of(lax.rem(k2y, 2) * 16, 16)
            block = grecv[k2y // 2, par, pl.ds(start, 16), :] * (1.0 / 16777216.0)
            tiled = jnp.concatenate([block] * 16, axis=0)
            top, rest = halves(jnp.where(own, tiled, 0.0))
            green[par] += dot_nn(top, pick) + dot_nn(rest, pick)
        return carry

    lax.fori_loop(0, 16, permute_green, 0)
    lax.fori_loop(0, 2 * CHUNKS, build_slopes, 0)

    forward.wait()

    fc, fs = (fc0[...], fc1[...]), (fs0[...], fs1[...])
    gc, gs = (gc0[...], gc1[...]), (gs0[...], gs1[...])
    lc, ls = (lc0[...], lc1[...]), (ls0[...], ls1[...])
    for par in range(2):
        at = 4 * par
        xr_ = halves(jnp.concatenate([rbuf[:, at, :], rbuf[:, at + 1, :]], axis=0))
        xi_ = halves(jnp.concatenate([rbuf[:, at + 2, :], rbuf[:, at + 3, :]], axis=0))
        ur = triple(dot_nn, fc, xr_) + triple(dot_nn, fs, xi_)
        ui = triple(dot_nn, fc, xi_) - triple(dot_nn, fs, xr_)
        tc, ts = twc[...], tws[...]
        vr = halves(ur * tc + ui * ts)
        vi = halves(ui * tc - ur * ts)
        g = green[par]
        er = halves(g * (triple(dot_nn, vr, lc) + triple(dot_nn, vi, ls)))
        ei = halves(g * (triple(dot_nn, vi, lc) - triple(dot_nn, vr, ls)))
        br = triple(dot_nt, er, lc) - triple(dot_nt, ei, ls)
        bi = triple(dot_nt, ei, lc) + triple(dot_nt, er, ls)
        hr = halves(br * tc - bi * ts)
        hi = halves(bi * tc + br * ts)
        tr = triple(dot_nn, gc, hr) - triple(dot_nn, gs, hi)
        ti = triple(dot_nn, gc, hi) + triple(dot_nn, gs, hr)
        for xh in range(2):
            tbuf[:, at + xh, :] = tr[128 * xh : 128 * xh + 128]
            tbuf[:, at + 2 + xh, :] = ti[128 * xh : 128 * xh + 128]

    backward = exchange(tbuf, qbuf, 5)
    backward.wait()

    for xh in range(2):
        qr = jnp.concatenate([qbuf[:, xh, :], qbuf[:, 4 + xh, :]], axis=0)
        qi = jnp.concatenate([qbuf[:, 2 + xh, :], qbuf[:, 6 + xh, :]], axis=0)
        qr, qi = halves(qr.T), halves(qi.T)
        lo = slice(256 * xh, 256 * xh + 256)
        pot[0, lo, :] = triple(dot_nn, qr, zc) - triple(dot_nn, qi, zs)
        pot[1, lo, :] = triple(dot_nn, qi, zc) + triple(dot_nn, qr, zs)

    for s in range(2):
        view = pot.at[s].reshape(32, 16, 256)
        for k in range(5):
            ys[s, 32 * k : 32 * k + 32] = view[:, 11 + k, :]
        for k in range(5):
            hal[s, 8 * k : 8 * k + 8] = view[27 + k, 8:16]
    edge = pot.at[:, 432:512, :]
    back_halo = [
        remote(ys, yb, 6, row, up_c),
        remote(edge, xb, 7, up_r, col),
        remote(hal.at[:, 0:CH], cb, 8, up_r, up_c),
    ]
    for copy in back_halo:
        copy.start()

    for s in range(2):
        top, rest = halves(pot[s])
        fint[s, :, 0:256] = top
        fint[s, :, 256:512] = rest

    for copy in back_halo:
        copy.wait()
    for s in range(2):
        for at, ref, n in ((0, yb, YH), (YH, xb, XH), (YH + XH, cb, CH)):
            top, rest = halves(ref[s])
            fhal[s, at : at + n, 0:256] = top
            fhal[s, at : at + n, 256:512] = rest

    def sample(ref, s, hi_ref, lo_ref, lanes):
        a = ref[s, :, 0:256], ref[s, :, 256:512]
        return triple(dot_nn, a, (hi_ref[s, :, lanes], lo_ref[s, :, lanes]))

    def gather(i, carry):
        s = i // GCHUNKS
        lanes = pl.ds(pl.multiple_of(lax.rem(i, GCHUNKS) * GCHUNK, GCHUNK), GCHUNK)
        plain = sample(fint, s, z_hi, z_lo, lanes)
        slope = sample(fint, s, sz_hi, sz_lo, lanes)
        a1 = a2 = a3 = jnp.zeros((16, GCHUNK), F32)
        for x in range(32):
            wx, sx = x_scr[s, x : x + 1, lanes], sx_scr[s, x : x + 1, lanes]
            part = plain[16 * x : 16 * x + 16]
            a1 = a1 + part * sx
            a2 = a2 + part * wx
            a3 = a3 + slope[16 * x : 16 * x + 16] * wx
        plain = sample(fhal, s, z_hi, z_lo, lanes)
        slope = sample(fhal, s, sz_hi, sz_lo, lanes)
        b1 = b2 = b3 = jnp.zeros((32, GCHUNK), F32)
        e1 = e2 = e3 = jnp.zeros((8, GCHUNK), F32)
        for k in range(5):
            wy, sy = y_scr[s, 19 + k : 20 + k, lanes], sy_scr[s, 19 + k : 20 + k, lanes]
            wx, sx = x_scr[s, 35 + k : 36 + k, lanes], sx_scr[s, 35 + k : 36 + k, lanes]
            part = plain[32 * k : 32 * k + 32]
            b1 = b1 + part * wy
            b2 = b2 + part * sy
            b3 = b3 + slope[32 * k : 32 * k + 32] * wy
            at = YH + 16 * k
            part = plain[at : at + 16]
            a1 = a1 + part * sx
            a2 = a2 + part * wx
            a3 = a3 + slope[at : at + 16] * wx
            at = YH + XH + 8 * k
            part = plain[at : at + 8]
            e1 = e1 + part * sx
            e2 = e2 + part * wx
            e3 = e3 + slope[at : at + 8] * wx
        wy, sy = y_scr[s, 0:16, lanes], sy_scr[s, 0:16, lanes]
        vy, ty = y_scr[s, 16:24, lanes], sy_scr[s, 16:24, lanes]
        wx, sx = x_scr[s, 0:32, lanes], sx_scr[s, 0:32, lanes]

        def total(a, m, e, n, b, q):
            parts = [a * m, e * n, b * q]
            return sum(jnp.sum(part, axis=0, keepdims=True) for part in parts)

        negative = -yq_scr[s, 24:25, lanes]
        forces[s, 0:1, lanes] = negative * total(a1, wy, e1, vy, b1, sx)
        forces[s, 1:2, lanes] = negative * total(a2, sy, e2, ty, b2, wx)
        forces[s, 2:3, lanes] = negative * total(a3, wy, e3, vy, b3, wx)
        return carry

    lax.fori_loop(0, 2 * GCHUNKS, gather, 0)


def shards(consts, cell_index, fraction, charge, atom_count, influence):
    vmem = pl.BlockSpec(memory_space=pltpu.VMEM)
    args = [cell_index, fraction, charge, atom_count, influence] + [jnp.asarray(c) for c in consts]
    v = pltpu.VMEM
    scratch = [
        v((2, 2, 6, 3, ATOMS), F32), v((2, 40, ATOMS), F32), v((2, 24, ATOMS), F32),
        v((2, 25, ATOMS), F32), v((2, 256, ATOMS), BF16), v((2, 256, ATOMS), BF16),
        v((2, 40, ATOMS), F32), v((2, 24, ATOMS), F32), v((2, 256, ATOMS), BF16),
        v((2, 256, ATOMS), BF16), v((512, CHUNK), BF16), v((512, CHUNK), BF16),
        v((2, HALO, 256), F32), v((2, YH, 256), F32), v((2, XH, 256), F32), v((2, CH, 256), F32),
        v((2, 512, 256), F32), v((ROWS, 2, 32, 256), F32), v((ROWS, 2, 32, 256), F32),
        v((2, 256, 256), F32), v((DEVS, 8, 256), F32), v((DEVS, 8, 256), F32),
        v((DEVS, 8, 256), F32), v((DEVS, 8, 256), F32), v((2, 512, 256), F32),
        v((2, YH, 256), F32), v((2, YH, 256), F32), v((2, XH, 256), F32), v((2, CH, 256), F32),
        v((2, 512, 512), BF16), v((2, HALO, 512), BF16),
        pltpu.SemaphoreType.DMA((18,)),
    ]
    return pl.pallas_call(
        kernel,
        out_shape=jax.ShapeDtypeStruct((2, 3, ATOMS), F32),
        in_specs=[vmem] * len(args),
        out_specs=vmem,
        scratch_shapes=scratch,
        compiler_params=pltpu.CompilerParams(
            collective_id=0, has_side_effects=True, vmem_limit_bytes=66_000_000
        ),
    )(*args)


def solution(mesh):
    placed = (
        P(None, None, ("row", "col")),
        P(None, None, ("row", "col")),
        P(None, ("row", "col")),
        P(None, ("row", "col")),
        P("row", "col", None),
    )
    return jax.shard_map(
        functools.partial(shards, tables()), mesh=mesh, in_specs=placed,
        out_specs=P(None, None, ("row", "col")), check_vma=False,
    )
```

profile of v0, /device:TPU:1, one launch (start us, length us, event | category | flops | bytes accessed | tf_op | source)
XLA Modules:
  0.0 101.0 jit_solution(14530982934662797792)
XLA Ops:
  0.0 1.3 %copy.26.count = s32[2,1]{1,0:T(2,128)} copy(s32[2,1]{0,1:T(1,128)} %param.26) | data formatting | bytes 16 | tf_op args[3]
  1.3 0.0 copy-start
  1.3 1.5 %copy.24.cell = s32[2,3,2048]{2,1,0:T(4,128)} copy(s32[2,3,2048]{2,0,1:T(2,128)} %param.23) | data formatting | bytes 98304 | tf_op args[0]
  2.8 0.0 copy-done
  2.8 0.7 copy.25.frac
  3.4 96.1 %shard_map.217 = f32[2,3,2048]{2,1,0:T(4,128)} custom-call(s32[2,3,2048]{2,1,0:T(4,128)} %copy.24.cell, f32[2,3,2048]{2,1,0:T(4,128)} %copy.25.frac, f32[2,2048]{1,0:T(2,128)} %charge.1, s32[2,1]{1,0:T(2,128)} %copy.26.count, f32[32,16,256]{2,1,0:T(8,128)} %infl.1, bf16[256,256]{1,0:T(8,128)(2,1)} %constant.36.clone.zc0, ...), custom_call_target="tpu_custom_call" | custom-call | tf_op jit(solution)/shard_map/pallas_call | solution.py:431
  99.5 1.5 %copy.27 = f32[2,3,2048]{2,0,1:T(2,128)} copy(f32[2,3,2048]{2,1,0:T(4,128)} %shard_map.217) | data formatting | bytes 98304 | tf_op jit(solution)/shard_map/pallas_call | solution.py:431
Async XLA Ops:
  1.3 1.5 %copy-start = (f32[2,3,2048]{2,0,1:T(2,128)S(1)}, f32[2,3,2048]{2,0,1:T(2,128)}, u32[]{:S(2)}) copy-start(f32[2,3,2048]{2,0,1:T(2,128)} %param.24) | copy-start | bytes 147460
where the time goes:
time: 101 us
  Pallas kernels  96.1 us (95%)
  local copies, waits for them, and re-layouts  4.91 us (5%)
    pallas_call x1, Pallas kernels, shards(): pl.pallas_call(kernel, out_shape=jax.ShapeDtypeStruct((2, 3, ATOMS), F32)...  96.1 us
    unnamed x5, local copies, waits for them, and re-layouts  3.41 us

commit v1 on v0

v1 whole, which is shorter than its diff:
```python
import functools

import jax
import jax.numpy as jnp
import numpy as np
from jax import lax
from jax.experimental import pallas as pl
from jax.experimental.pallas import tpu as pltpu
from jax.sharding import PartitionSpec as P

F32 = jnp.float32
BF16 = jnp.bfloat16
MESH = pl.DeviceIdType.MESH

K = 256
ROWS = 8
COLS = 16
DEVS = ROWS * COLS
ATOMS = 2048
CHUNK = 512
CHUNKS = ATOMS // CHUNK
GCHUNK = 256
GCHUNKS = ATOMS // GCHUNK

YH, XH, CH = 160, 80, 48
HALO = YH + XH + CH
OFFSETS = sorted(
    (d for d in np.ndindex(4, 4, 4, 2) if d != (0, 0, 0, 0)),
    key=lambda d: (-sum(min(k, 4 - k) for k in d[:3]), d[3], d[0] + 2 * d[1] + 3 * d[2]),
)


def halves(x):
    top = x.astype(BF16)
    return top, (x - top.astype(F32)).astype(BF16)


def np_halves(x):
    x = np.asarray(x, np.float32)
    top = x.astype(jnp.bfloat16)
    return [top, (x - top.astype(np.float32)).astype(jnp.bfloat16)]


def tables():
    d = np.arange(DEVS)
    waves = np.concatenate([16 * (d % COLS) + 2 * (d // COLS) + p for p in range(2)])
    turn = 2.0 * np.pi / K
    angle = (waves[:, None] * np.arange(K)[None, :] % K) * turn
    out = np_halves(np.cos(angle)) + np_halves(np.sin(angle))
    spot = np.arange(256)
    rx, cc = 2 * (spot % 128 // 16) + spot // 128, spot % 16
    angle = ((rx[:, None] * rx[None, :] + cc[:, None] * cc[None, :]) % 16) * (16 * turn)
    out += np_halves(np.cos(angle)) + np_halves(np.sin(angle))
    xl, yl = spot // 16, spot % 16
    angle = ((xl[:, None] * xl[None, :] + yl[:, None] * yl[None, :]) % 16) * (16 * turn)
    out += np_halves(np.cos(angle)) + np_halves(np.sin(angle))
    angle = ((rx[:, None] * xl[None, :] + cc[:, None] * yl[None, :]) % K) * turn
    twiddles = np.stack([np.cos(angle), np.sin(angle)]).astype(np.float32)
    return np.stack(out), twiddles


def spline_values(f):
    nothing = jnp.zeros_like(f)
    levels = [f, 1.0 - f]
    slopes = levels
    for degree in range(3, 7):
        padded = levels + [nothing]
        following = []
        for o in range(degree):
            value = (f + float(o)) * padded[o]
            if o > 0:
                value = value + (float(degree - o) - f) * padded[o - 1]
            following.append(value * (1.0 / (degree - 1)))
        if degree == 6:
            slopes = [padded[0]] + [padded[o] - padded[o - 1] for o in range(1, 6)]
        levels = following
    return levels, slopes


def dot_nn(a, b):
    return lax.dot_general(a, b, (((1,), (0,)), ((), ())), preferred_element_type=F32)


def dot_nt(a, b):
    return lax.dot_general(a, b, (((1,), (1,)), ((), ())), preferred_element_type=F32)


def triple_nn(a, b):
    left = jnp.concatenate([a[0], a[1], a[0]], axis=1)
    return dot_nn(left, jnp.concatenate([b[0], b[0], b[1]], axis=0))


def triple_nt(a, b):
    left = jnp.concatenate([a[0], a[1], a[0]], axis=1)
    return dot_nt(left, jnp.concatenate([b[0], b[0], b[1]], axis=1))


def dense(gap, rows):
    total = jnp.where(gap == 0, rows[0], 0.0)
    for j in range(1, 6):
        total = jnp.where(gap == j, rows[j], total)
    return total


def kernel(
    cell, frac, charge, count, infl_hbm, tab_hbm, twid_hbm,
    forces,
    infl, tab, twid, w_scr, x_scr, y_scr, yq_scr, z_hi, z_lo, sx_scr, sy_scr, sz_hi, sz_lo,
    p_hi, p_lo, hal, yr, xr, cr, mesh, gsend, grecv, green, wb, fb, gb, lb,
    sbuf, rbuf, tbuf, qbuf, pot, ys, yb, xb, cb, fint, fhal, part, swap,
    sems, local, gate,
):
    row = lax.axis_index("row")
    col = lax.axis_index("col")
    me = row * COLS + col
    up_r, dn_r = lax.rem(row + 1, ROWS), lax.rem(row + ROWS - 1, ROWS)
    up_c, dn_c = lax.rem(col + 1, COLS), lax.rem(col + COLS - 1, COLS)
    core = lax.rem(col, 2)
    px = lax.rem(lax.div(col, 2), 2) * 2 + lax.rem(row, 2)
    py, pz = lax.div(col, 4), lax.div(row, 2)

    xs = [lax.rem(px + d, 4) for d in range(4)]
    x_row, x_col = [lax.rem(x, 2) for x in xs], [lax.div(x, 2) * 2 for x in xs]
    y_col = [lax.rem(py + d, 4) * 4 for d in range(4)]
    z_row = [lax.rem(pz + d, 4) * 2 for d in range(4)]
    cores = core, 1 - core

    def device(dx, dy, dz, dc):
        return z_row[dz] + x_row[dx], y_col[dy] + x_col[dx] + cores[dc]

    loads = [
        pltpu.make_async_copy(infl_hbm, infl, local.at[0]),
        pltpu.make_async_copy(tab_hbm, tab, local.at[1]),
        pltpu.make_async_copy(twid_hbm, twid, local.at[2]),
    ]
    for copy in loads:
        copy.start()

    barrier = pltpu.get_barrier_semaphore()

    def greet_column(k, carry):
        to = row, lax.rem(col + k, COLS)
        pl.semaphore_signal(barrier, inc=1, device_id=to, device_id_type=MESH)
        return carry

    def greet_row(k, carry):
        to = lax.rem(row + k, ROWS), col
        pl.semaphore_signal(barrier, inc=1, device_id=to, device_id_type=MESH)
        return carry

    def vouch(k, carry):
        to = lax.rem(row + k, ROWS), col
        pl.semaphore_signal(gate, inc=1, device_id=to, device_id_type=MESH)
        return carry

    lax.fori_loop(1, ROWS, greet_row, 0)
    lax.fori_loop(1, COLS, greet_column, 0)

    def remote(src, dst, send, recv, to):
        return pltpu.make_async_remote_copy(
            src_ref=src, dst_ref=dst, send_sem=sems.at[send], recv_sem=sems.at[recv],
            device_id=to, device_id_type=MESH,
        )

    slot = lax.broadcasted_iota(jnp.int32, (1, ATOMS), 1)
    values, slopes = spline_values(jnp.concatenate([frac[0], frac[1], frac[2]], axis=0))
    for j in range(6):
        w_scr[0, j] = values[j]
        w_scr[1, j] = slopes[j]
    for s in range(2):
        yq_scr[s, 24:25] = jnp.where(slot < count[0:1, s : s + 1], charge[s : s + 1], 0.0)

    loads[0].wait()
    for k in range(16):
        gsend[k // 2, k % 2] = infl[:, k, :]
    pl.semaphore_wait(barrier, ROWS + COLS - 2)
    lax.fori_loop(1, ROWS, vouch, 0)

    def send_green(k, carry):
        there = lax.rem(row + k, ROWS)
        remote(gsend.at[there], grecv.at[row], 0, 1, (there, col)).start()
        return carry

    lax.fori_loop(1, ROWS, send_green, 0)
    grecv[row] = gsend[row]

    def spans(i):
        s = lax.div(i, CHUNKS)
        return s, pl.ds(pl.multiple_of(lax.rem(i, CHUNKS) * CHUNK, CHUNK), CHUNK)

    def positions(n, near):
        spot = lax.broadcasted_iota(jnp.int32, (n, CHUNK), 0)
        return jnp.where(spot < near, spot, spot - n)

    def rows_of(s, kind, dim, lanes):
        return [w_scr[kind, j, pl.ds(2 * dim + s, 1), lanes] for j in range(6)]

    def gaps(s, lanes):
        return (
            (cell[0, pl.ds(s, 1), lanes] - row * 32) - positions(40, 32),
            (cell[1, pl.ds(s, 1), lanes] - col * 16) - positions(24, 16),
            (cell[2, pl.ds(s, 1), lanes] - positions(256, 256)) & 255,
        )

    def build(i, carry):
        s, lanes = spans(i)
        gx, gy, gz = gaps(s, lanes)
        x_scr[s, :, lanes] = dense(gx, rows_of(s, 0, 0, lanes))
        y = dense(gy, rows_of(s, 0, 1, lanes))
        y_scr[s, :, lanes] = y
        yq_scr[s, 0:24, lanes] = y * yq_scr[s, 24:25, lanes]
        top, rest = halves(dense(gz, rows_of(s, 0, 2, lanes)))
        z_hi[s, :, lanes] = top
        z_lo[s, :, lanes] = rest
        return carry

    def build_slopes(i, carry):
        s, lanes = spans(i)
        gx, gy, gz = gaps(s, lanes)
        sx_scr[s, :, lanes] = dense(gx, rows_of(s, 1, 0, lanes))
        sy_scr[s, :, lanes] = dense(gy, rows_of(s, 1, 1, lanes))
        top, rest = halves(dense(gz, rows_of(s, 1, 2, lanes)))
        sz_hi[s, :, lanes] = top
        sz_lo[s, :, lanes] = rest
        return carry

    lax.fori_loop(0, 2 * CHUNKS, build, 0)

    def put(at, value):
        top, rest = halves(value)
        p_hi[at : at + value.shape[0], :] = top
        p_lo[at : at + value.shape[0], :] = rest

    def accumulate(ref, s, lanes, n):
        a = p_hi[0:n, :], p_lo[0:n, :]
        b = z_hi[s, :, lanes], z_lo[s, :, lanes]
        ref[s] += triple_nt(a, b)

    def halo_chunk(i, carry):
        s, lanes = spans(i)
        for k in range(5):
            put(32 * k, x_scr[s, 0:32, lanes] * yq_scr[s, 19 + k : 20 + k, lanes])
        for k in range(5):
            put(YH + 16 * k, yq_scr[s, 0:16, lanes] * x_scr[s, 35 + k : 36 + k, lanes])
        edge = yq_scr[s, 16:24, lanes]
        for k in range(3):
            first = edge * x_scr[s, 35 + 2 * k : 36 + 2 * k, lanes]
            if k < 2:
                second = edge * x_scr[s, 36 + 2 * k : 37 + 2 * k, lanes]
            else:
                second = jnp.zeros_like(first)
            put(YH + XH + 16 * k, jnp.concatenate([first, second], axis=0))
        accumulate(hal, s, lanes, HALO)
        return carry

    hal[...] = jnp.zeros_like(hal)
    edges = []
    for s in range(2):
        lax.fori_loop(s * CHUNKS, (s + 1) * CHUNKS, halo_chunk, 0)
        if s == 0:
            pl.semaphore_wait(gate, ROWS - 1)
        at = 2 + 6 * s
        edges += [
            remote(hal.at[s, 0:YH], yr.at[s], at, at + 1, (row, dn_c)),
            remote(hal.at[s, YH : YH + XH], xr.at[s], at + 2, at + 3, (dn_r, col)),
            remote(hal.at[s, YH + XH : HALO], cr.at[s], at + 4, at + 5, (dn_r, dn_c)),
        ]
        for copy in edges[3 * s :]:
            copy.start()

    lax.fori_loop(0, 2 * CHUNKS, build_slopes, 0)

    def inner_chunk(i, carry):
        s, lanes = spans(i)
        for x in range(32):
            put(16 * x, yq_scr[s, 0:16, lanes] * x_scr[s, x : x + 1, lanes])
        accumulate(mesh, s, lanes, 512)
        return carry

    mesh[...] = jnp.zeros_like(mesh)
    lax.fori_loop(0, 2 * CHUNKS, inner_chunk, 0)

    for copy in loads[1:]:
        copy.wait()
    for h in range(2):
        zc, zs, fc, fs, lc, ls = [tab[2 * k + h] for k in range(6)]
        for par in range(2):
            at = slice(128 * par, 128 * par + 128)
            wb[h, par, 0:128, 0:256] = zc[at]
            wb[h, par, 0:128, 256:512] = zs[at]
            wb[h, par, 128:256, 0:256] = -zs[at]
            wb[h, par, 128:256, 256:512] = zc[at]
        for ref, c, s in ((fb, fc, fs), (gb, fc, -fs), (lb, lc, -ls)):
            ref[h, 0:256, 0:256] = c
            ref[h, 0:256, 256:512] = s
            ref[h, 256:512, 0:256] = -s
            ref[h, 256:512, 256:512] = c

    remote(gsend.at[0 : ROWS - 1], grecv.at[0 : ROWS - 1], 0, 1, (up_r, col)).wait()
    lane = lax.broadcasted_iota(jnp.int32, (16, 256), 1)

    def trade(par, bits, load, store):
        for rest in range(4):
            base = [(a << bits[0]) + (b << bits[1]) + (rest << (2 if bits[0] == 0 else 0))
                    for b in range(2) for a in range(2)]
            blocks = [load(k) for k in base]
            for i, bit in enumerate(bits):
                step = 1 << bit
                low = (lane & step) == 0
                for k in range(4):
                    if k & (1 << i):
                        continue
                    a, b = blocks[k], blocks[k | (1 << i)]
                    blocks[k] = jnp.where(low, a, pltpu.roll(b, step, 1))
                    blocks[k | (1 << i)] = jnp.where(low, pltpu.roll(a, 256 - step, 1), b)
            for k, block in zip(base, blocks):
                store(k, block)

    def first_load(par, k):
        return grecv[k // 2, par, 16 * (k % 2) : 16 * (k % 2) + 16, :] * (1.0 / 16777216.0)

    def first_store(par, k, block):
        swap[par, 16 * k : 16 * k + 16, :] = block

    def last_store(par, k, block):
        at = 128 * (k % 2) + 16 * (k // 2)
        green[par, at : at + 16, :] = block

    for par in range(2):
        trade(par, (0, 1), functools.partial(first_load, par), functools.partial(first_store, par))
        trade(par, (2, 3), lambda k: swap[par, 16 * k : 16 * k + 16, :],
              functools.partial(last_store, par))

    for copy in edges:
        copy.wait()
    for s in range(2):
        view = mesh.at[s].reshape(32, 16, 256)
        for k in range(5):
            view[:, 11 + k, :] += yr[s, 32 * k : 32 * k + 32]
        for k in range(5):
            view[27 + k] += xr[s, 16 * k : 16 * k + 16]
            view[27 + k, 8:16] += cr[s, 8 * k : 8 * k + 8]

    class Exchange:
        def __init__(self, src, dst, par, first):
            self.src, self.dst, self.first = src.at[par], dst.at[par], first

        def start(self):
            for offset in OFFSETS:
                to = device(*offset)
                src = self.src.at[to[0] * COLS + to[1]]
                remote(src, self.dst.at[me], self.first, self.first + 1, to).start()
            self.dst[me] = self.src[me]

        def wait(self):
            every = slice(0, DEVS - 1)
            remote(
                self.src.at[every], self.dst.at[every], self.first, self.first + 1, (up_r, col)
            ).wait()

    tops = [halves(jnp.concatenate([mesh[0, q, :], mesh[1, q, :]], axis=1))
            for q in (slice(0, 256), slice(256, 512))]
    forward = [Exchange(sbuf, rbuf, par, 14 + 2 * par) for par in range(2)]
    for par in range(2):
        for xh in range(2):
            a = triple_nt((wb[0, par], wb[1, par]), tops[xh])
            for reim in range(2):
                for lh in range(2):
                    sbuf[par, :, 4 * reim + 2 * xh + lh, :] = a[
                        128 * reim : 128 * reim + 128, 128 * lh : 128 * lh + 128
                    ]
        forward[par].start()

    fbig, gbig, lbig = (fb[0], fb[1]), (gb[0], gb[1]), (lb[0], lb[1])
    tc, ts = twid[0], twid[1]

    def stacked(buf, par):
        parts = [
            jnp.concatenate([buf[par, :, 2 * j, :], buf[par, :, 2 * j + 1, :]], axis=1)
            for j in range(4)
        ]
        return jnp.concatenate(parts, axis=0)

    backward = [Exchange(tbuf, qbuf, par, 18 + 2 * par) for par in range(2)]
    for par in range(2):
        forward[par].wait()
        u = triple_nn(fbig, halves(stacked(rbuf, par)))
        ur, ui = u[0:256], u[256:512]
        v = jnp.concatenate([ur * tc + ui * ts, ui * tc - ur * ts], axis=1)
        g = jnp.concatenate([green[par], green[par]], axis=1)
        e = g * triple_nn(halves(v), lbig)
        b = triple_nt(halves(e), lbig)
        br, bi = b[:, 0:256], b[:, 256:512]
        h = jnp.concatenate([br * tc - bi * ts, bi * tc + br * ts], axis=0)
        t = triple_nn(gbig, halves(h))
        for j in range(4):
            for lh in range(2):
                tbuf[par, :, 2 * j + lh, :] = t[
                    128 * j : 128 * j + 128, 128 * lh : 128 * lh + 128
                ]
        backward[par].start()

    for par in range(2):
        backward[par].wait()
        q = stacked(qbuf, par)
        w = wb[0, par], wb[1, par]
        for xh in range(2):
            picked = jnp.concatenate(
                [q[128 * xh : 128 * xh + 128], q[256 + 128 * xh : 384 + 128 * xh]], axis=0
            )
            a = triple_nn(halves(picked.T), w)
            lo = slice(256 * xh, 256 * xh + 256)
            for s in range(2):
                value = a[:, 256 * s : 256 * s + 256]
                pot[s, lo, :] = value if par == 0 else pot[s, lo, :] + value

    for s in range(2):
        view = pot.at[s].reshape(32, 16, 256)
        for k in range(5):
            ys[s, 32 * k : 32 * k + 32] = view[:, 11 + k, :]
        for k in range(5):
            hal[s, 8 * k : 8 * k + 8] = view[27 + k, 8:16]
    back_halo = [
        remote(ys, yb, 22, 23, (row, up_c)),
        remote(pot.at[:, 432:512, :], xb, 24, 25, (up_r, col)),
        remote(hal.at[:, 0:CH], cb, 26, 27, (up_r, up_c)),
    ]
    for copy in back_halo:
        copy.start()

    def spread_out(ref, s, at, value):
        top, rest = halves(value)
        n = value.shape[0]
        ref[s, at : at + n, 0:256] = top
        ref[s, at : at + n, 256:512] = rest
        ref[s, at : at + n, 512:768] = top

    def sample(ref, s, lanes):
        top = jnp.concatenate([z_hi[s, :, lanes], sz_hi[s, :, lanes]], axis=1)
        rest = jnp.concatenate([z_lo[s, :, lanes], sz_lo[s, :, lanes]], axis=1)
        both = dot_nn(ref[s], jnp.concatenate([top, top, rest], axis=0))
        return both[:, 0:GCHUNK], both[:, GCHUNK : 2 * GCHUNK]

    def window(i):
        s = lax.div(i, GCHUNKS)
        return s, pl.ds(pl.multiple_of(lax.rem(i, GCHUNKS) * GCHUNK, GCHUNK), GCHUNK)

    def down(value):
        return jnp.sum(value, axis=0, keepdims=True)

    def gather_inner(i, carry):
        s, lanes = window(i)
        plain, slope = sample(fint, s, lanes)
        a1 = a2 = a3 = jnp.zeros((16, GCHUNK), F32)
        for x in range(32):
            wx, sx = x_scr[s, x : x + 1, lanes], sx_scr[s, x : x + 1, lanes]
            piece = plain[16 * x : 16 * x + 16]
            a1 = a1 + piece * sx
            a2 = a2 + piece * wx
            a3 = a3 + slope[16 * x : 16 * x + 16] * wx
        wy, sy = y_scr[s, 0:16, lanes], sy_scr[s, 0:16, lanes]
        part[s, 0:1, lanes] = down(a1 * wy)
        part[s, 1:2, lanes] = down(a2 * sy)
        part[s, 2:3, lanes] = down(a3 * wy)
        return carry

    def gather_halo(i, carry):
        s, lanes = window(i)
        plain, slope = sample(fhal, s, lanes)
        a1 = a2 = a3 = jnp.zeros((16, GCHUNK), F32)
        b1 = b2 = b3 = jnp.zeros((32, GCHUNK), F32)
        e1 = e2 = e3 = jnp.zeros((8, GCHUNK), F32)
        for k in range(5):
            wy, sy = y_scr[s, 19 + k : 20 + k, lanes], sy_scr[s, 19 + k : 20 + k, lanes]
            wx, sx = x_scr[s, 35 + k : 36 + k, lanes], sx_scr[s, 35 + k : 36 + k, lanes]
            piece = plain[32 * k : 32 * k + 32]
            b1 = b1 + piece * wy
            b2 = b2 + piece * sy
            b3 = b3 + slope[32 * k : 32 * k + 32] * wy
            at = YH + 16 * k
            piece = plain[at : at + 16]
            a1 = a1 + piece * sx
            a2 = a2 + piece * wx
            a3 = a3 + slope[at : at + 16] * wx
            at = YH + XH + 8 * k
            piece = plain[at : at + 8]
            e1 = e1 + piece * sx
            e2 = e2 + piece * wx
            e3 = e3 + slope[at : at + 8] * wx
        wy, sy = y_scr[s, 0:16, lanes], sy_scr[s, 0:16, lanes]
        vy, ty = y_scr[s, 16:24, lanes], sy_scr[s, 16:24, lanes]
        wx, sx = x_scr[s, 0:32, lanes], sx_scr[s, 0:32, lanes]

        def finish(d, a, m, e, n, b, q):
            total = part[s, d : d + 1, lanes] + down(a * m) + down(e * n) + down(b * q)
            forces[d, pl.ds(s, 1), lanes] = -yq_scr[s, 24:25, lanes] * total

        finish(0, a1, wy, e1, vy, b1, sx)
        finish(1, a2, sy, e2, ty, b2, wx)
        finish(2, a3, wy, e3, vy, b3, wx)
        return carry

    for s in range(2):
        spread_out(fint, s, 0, pot[s])
    lax.fori_loop(0, 2 * GCHUNKS, gather_inner, 0)

    for copy in back_halo:
        copy.wait()
    for s in range(2):
        for at, ref in ((0, yb), (YH, xb), (YH + XH, cb)):
            spread_out(fhal, s, at, ref[s])

    lax.fori_loop(0, 2 * GCHUNKS, gather_halo, 0)


def shards(consts, cell_index, fraction, charge, atom_count, influence):
    vmem = pl.BlockSpec(memory_space=pltpu.VMEM)
    anywhere = pl.BlockSpec(memory_space=pl.ANY)
    args = [
        jnp.transpose(cell_index, (1, 0, 2)), jnp.transpose(fraction, (1, 0, 2)), charge,
        jnp.transpose(atom_count), influence, jnp.asarray(consts[0]), jnp.asarray(consts[1]),
    ]
    v = pltpu.VMEM
    scratch = [
        v((32, 16, 256), F32), v((12, 256, 256), BF16), v((2, 256, 256), F32),
        v((2, 6, 6, ATOMS), F32), v((2, 40, ATOMS), F32), v((2, 24, ATOMS), F32),
        v((2, 25, ATOMS), F32), v((2, 256, ATOMS), BF16), v((2, 256, ATOMS), BF16),
        v((2, 40, ATOMS), F32), v((2, 24, ATOMS), F32), v((2, 256, ATOMS), BF16),
        v((2, 256, ATOMS), BF16), v((512, CHUNK), BF16), v((512, CHUNK), BF16),
        v((2, HALO, 256), F32), v((2, YH, 256), F32), v((2, XH, 256), F32), v((2, CH, 256), F32),
        v((2, 512, 256), F32),
        v((ROWS, 2, 32, 256), F32), v((ROWS, 2, 32, 256), F32), v((2, 256, 256), F32),
        v((2, 2, 256, 512), BF16), v((2, 512, 512), BF16), v((2, 512, 512), BF16),
        v((2, 512, 512), BF16),
        v((2, DEVS, 8, 128), F32), v((2, DEVS, 8, 128), F32), v((2, DEVS, 8, 128), F32),
        v((2, DEVS, 8, 128), F32), v((2, 512, 256), F32),
        v((2, YH, 256), F32), v((2, YH, 256), F32), v((2, XH, 256), F32), v((2, CH, 256), F32),
        v((2, 512, 768), BF16), v((2, HALO, 768), BF16), v((2, 3, ATOMS), F32),
        v((2, 256, 256), F32),
        pltpu.SemaphoreType.DMA((28,)), pltpu.SemaphoreType.DMA((3,)), pltpu.SemaphoreType.REGULAR,
    ]
    out = pl.pallas_call(
        kernel,
        out_shape=jax.ShapeDtypeStruct((3, 2, ATOMS), F32),
        in_specs=[vmem] * 4 + [anywhere] * 3,
        out_specs=vmem,
        scratch_shapes=scratch,
        compiler_params=pltpu.CompilerParams(
            collective_id=0, has_side_effects=True, vmem_limit_bytes=66_000_000
        ),
    )(*args)
    return jnp.transpose(out, (1, 0, 2))


def solution(mesh):
    placed = (
        P(None, None, ("row", "col")),
        P(None, None, ("row", "col")),
        P(None, ("row", "col")),
        P(None, ("row", "col")),
        P("row", "col", None),
    )
    return jax.shard_map(
        functools.partial(shards, tables()), mesh=mesh, in_specs=placed,
        out_specs=P(None, None, ("row", "col")), check_vma=False,
    )
```

time: 101 us -> 78.9 us (0.78)
  Pallas kernels: 96.1 us -> 77.2 us
  local copies, waits for them, and re-layouts: 4.91 us -> 1.42 us
    pallas_call x1, Pallas kernels: 96.1 us -> 77.2 us  [shards(): pl.pallas_call(kernel, out_shape=jax.ShapeDtypeStruct((3, 2, ATOMS), F32)...]
    unnamed x5 -> x1, local copies, waits for them, and re-layouts: 3.41 us -> 1.42 us
    pallas_call x1 -> x0, local copies, waits for them, and re-layouts: 1.5 us -> none  [shards(): pl.pallas_call(kernel, out_shape=jax.ShapeDtypeStruct((2, 3, ATOMS), F32)...]
where the time goes in v1:
time: 78.9 us; the launch traced here: 78.6 us
  Pallas kernels  77.2 us (98%)
  local copies, waits for them, and re-layouts  1.42 us (2%)
    pallas_call x1, Pallas kernels, shards(): pl.pallas_call(kernel, out_shape=jax.ShapeDtypeStruct((3, 2, ATOMS), F32)...  77.2 us

profile of v1, /device:TPU:1, one launch (start us, length us, event | category | flops | bytes accessed | tf_op | source)
XLA Modules:
  0.0 78.6 jit_solution(17430834453652654070)
XLA Ops:
  0.0 77.2 %shard_map.73 = f32[3,2,2048]{2,1,0:T(2,128)} custom-call(s32[3,2,2048]{2,1,0:T(2,128)} %bitcast.5, f32[3,2,2048]{2,1,0:T(2,128)} %bitcast.6, f32[2,2048]{1,0:T(2,128)} %charge.1, s32[1,2]{1,0:T(1,128)} %bitcast.7, f32[32,16,256]{2,1,0:T(8,128)} %infl_hbm.1, bf16[12,256,256]{2,1,0:T(8,128)(2,1)} %constant.4.clone.tab_hbm, f32[2,256,256]{2,1,0:T(8,128)} %constant.5.clone.twid_hbm), custom_call_target="tpu_custom_call" | custom-call | tf_op jit(solution)/shard_map/pallas_call | solution.py:542
  77.2 1.4 %copy.9 = f32[2,3,2048]{2,0,1:T(2,128)} copy(f32[2,3,2048]{2,0,1:T(2,128)} %bitcast.4) | data formatting | bytes 98304

commit v2 on v1

v2 whole, which is shorter than its diff:
```python
import functools

import jax
import jax.numpy as jnp
import numpy as np
from jax import lax
from jax.experimental import pallas as pl
from jax.experimental.pallas import tpu as pltpu
from jax.sharding import PartitionSpec as P

F32 = jnp.float32
BF16 = jnp.bfloat16
MESH = pl.DeviceIdType.MESH

K = 256
ROWS = 8
COLS = 16
DEVS = ROWS * COLS
ATOMS = 2048
CHUNK = 512
CHUNKS = ATOMS // CHUNK
GCHUNK = 256
GCHUNKS = ATOMS // GCHUNK

YH, XH, CH = 160, 80, 48
HALO = YH + XH + CH
MESH_ROWS = 592


def far_first():
    offsets = [d for d in np.ndindex(4, 4, 4, 2) if d != (0, 0, 0, 0)]
    offsets.sort(key=lambda d: (-sum(min(k, 4 - k) for k in d[:3]), d[3], d[0] + 2 * d[1] + 3 * d[2]))
    lanes = {}
    for d in offsets:
        lanes.setdefault(d[0] or 10 + d[1] if d[0] or d[1] else 20 + d[2], []).append(d)
    out = []
    while any(lanes.values()):
        out += [lane.pop(0) for lane in lanes.values() if lane]
    return out


OFFSETS = far_first()


def halves(x):
    top = x.astype(BF16)
    return top, (x - top.astype(F32)).astype(BF16)


def np_halves(x):
    x = np.asarray(x, np.float32)
    top = x.astype(jnp.bfloat16)
    return [top, (x - top.astype(np.float32)).astype(jnp.bfloat16)]


def tables():
    d = np.arange(DEVS)
    waves = 16 * (d % COLS) + 2 * (d // COLS) + (d % COLS >= COLS // 2)
    turn = 2.0 * np.pi / K
    angle = (waves[:, None] * np.arange(K)[None, :] % K) * turn
    sines = -np.sin(angle)
    sines[0] = 1.0 - 2.0 * (np.arange(K) % 2)
    out = np_halves(np.concatenate([np.cos(angle), sines]))
    spot = np.arange(256)
    rx, cc = 2 * (spot % 128 // 16) + spot // 128, spot % 16
    angle = ((rx[:, None] * rx[None, :] + cc[:, None] * cc[None, :]) % 16) * (16 * turn)
    out += np_halves(np.cos(angle)) + np_halves(np.sin(angle))
    xl, yl = spot // 16, spot % 16
    angle = ((xl[:, None] * xl[None, :] + yl[:, None] * yl[None, :]) % 16) * (16 * turn)
    out += np_halves(np.cos(angle)) + np_halves(np.sin(angle))
    angle = ((rx[:, None] * xl[None, :] + cc[:, None] * yl[None, :]) % K) * turn
    twiddles = np.stack([np.cos(angle), np.sin(angle)]).astype(np.float32)
    return np.stack(out), twiddles


def spline_values(f):
    nothing = jnp.zeros_like(f)
    levels = [f, 1.0 - f]
    slopes = levels
    for degree in range(3, 7):
        padded = levels + [nothing]
        following = []
        for o in range(degree):
            value = (f + float(o)) * padded[o]
            if o > 0:
                value = value + (float(degree - o) - f) * padded[o - 1]
            following.append(value * (1.0 / (degree - 1)))
        if degree == 6:
            slopes = [padded[0]] + [padded[o] - padded[o - 1] for o in range(1, 6)]
        levels = following
    return levels, slopes


def dot_nn(a, b):
    return lax.dot_general(a, b, (((1,), (0,)), ((), ())), preferred_element_type=F32)


def dot_nt(a, b):
    return lax.dot_general(a, b, (((1,), (1,)), ((), ())), preferred_element_type=F32)


def triple_nn(a, b):
    left = jnp.concatenate([a[0], a[1], a[0]], axis=1)
    return dot_nn(left, jnp.concatenate([b[0], b[0], b[1]], axis=0))


def triple_nt(a, b):
    left = jnp.concatenate([a[0], a[1], a[0]], axis=1)
    return dot_nt(left, jnp.concatenate([b[0], b[0], b[1]], axis=1))


def dense(gap, rows):
    total = jnp.where(gap == 0, rows[0], 0.0)
    for j in range(1, 6):
        total = jnp.where(gap == j, rows[j], total)
    return total


def tiles_of(anchor, rows, size):
    gap = anchor - lax.broadcasted_iota(jnp.int32, (size, anchor.shape[1]), 0)
    return dense(gap & (size - 1), rows), gap >> (3 if size == 8 else 4)


def kernel(
    cell, frac, charge, count, infl_hbm, tab_hbm, twid_hbm,
    forces,
    infl, tab, twid, w_scr, x_scr, y_scr, yq_scr, z_hi, z_lo, sx_scr, sy_scr, sz_hi, sz_lo,
    p_hi, p_lo, ncell, nfrac, qs, nq, nw_scr, nx_scr, nyq_scr, nz_hi, nz_lo, nacc, xr, mesh, gsend, grecv, glast, green, fb, gb, lb, escr,
    sbuf, rbuf, tbuf, qbuf, pot, ys, corner, yb, xb, cb, fint, fhal, part, swap, gone,
    sems, local, gate,
):
    row = lax.axis_index("row")
    col = lax.axis_index("col")
    me = row * COLS + col
    up_r, dn_r = lax.rem(row + 1, ROWS), lax.rem(row + ROWS - 1, ROWS)
    up_c, dn_c = lax.rem(col + 1, COLS), lax.rem(col + COLS - 1, COLS)
    core = lax.rem(col, 2)
    px = lax.rem(lax.div(col, 2), 2) * 2 + lax.rem(row, 2)
    py, pz = lax.div(col, 4), lax.div(row, 2)

    xs = [lax.rem(px + d, 4) for d in range(4)]
    x_row, x_col = [lax.rem(x, 2) for x in xs], [lax.div(x, 2) * 2 for x in xs]
    y_col = [lax.rem(py + d, 4) * 4 for d in range(4)]
    z_row = [lax.rem(pz + d, 4) * 2 for d in range(4)]
    cores = core, 1 - core

    def device(dx, dy, dz, dc):
        return z_row[dz] + x_row[dx], y_col[dy] + x_col[dx] + cores[dc]

    loads = [
        pltpu.make_async_copy(infl_hbm, infl, local.at[0]),
        pltpu.make_async_copy(tab_hbm, tab, local.at[1]),
        pltpu.make_async_copy(twid_hbm, twid, local.at[2]),
    ]
    for copy in loads:
        copy.start()

    barrier = pltpu.get_barrier_semaphore()

    def greet_column(k, carry):
        to = row, lax.rem(col + k, COLS)
        pl.semaphore_signal(barrier, inc=1, device_id=to, device_id_type=MESH)
        return carry

    def greet_row(k, carry):
        to = lax.rem(row + k, ROWS), col
        pl.semaphore_signal(barrier, inc=1, device_id=to, device_id_type=MESH)
        return carry

    def vouch(k, carry):
        to = lax.rem(row + k, ROWS), col
        pl.semaphore_signal(gate, inc=1, device_id=to, device_id_type=MESH)
        return carry

    lax.fori_loop(1, ROWS, greet_row, 0)
    lax.fori_loop(1, COLS, greet_column, 0)

    def remote(src, dst, send, recv, to):
        return pltpu.make_async_remote_copy(
            src_ref=src, dst_ref=dst, send_sem=sems.at[send], recv_sem=sems.at[recv],
            device_id=to, device_id_type=MESH,
        )

    slot = lax.broadcasted_iota(jnp.int32, (1, ATOMS), 1)
    values, slopes = spline_values(jnp.concatenate([frac[0], frac[1], frac[2]], axis=0))
    for j in range(6):
        w_scr[0, j] = values[j]
        w_scr[1, j] = slopes[j]
    for s in range(2):
        masked = jnp.where(slot < count[0:1, s : s + 1], charge[s : s + 1], 0.0)
        yq_scr[s, 24:25] = masked
        qs[s : s + 1] = masked

    loads[0].wait()
    late = jnp.full((32, 256), col >= COLS // 2)
    for k in range(ROWS):
        gsend[k] = jnp.where(late, infl[:, 2 * k + 1, :], infl[:, 2 * k, :])
    pl.semaphore_wait(barrier, ROWS + COLS - 2)
    lax.fori_loop(1, ROWS, vouch, 0)
    atoms = [
        remote(src, dst, 2 + 2 * k, 3 + 2 * k, (row, dn_c))
        for k, (src, dst) in enumerate(((cell, ncell), (frac, nfrac), (qs, nq)))
    ]
    for copy in atoms:
        copy.start()

    def send_green(k, carry):
        there = lax.rem(row + k, ROWS)
        remote(gsend.at[there], grecv.at[row], 0, 1, (there, col)).start()
        return carry

    lax.fori_loop(1, ROWS, send_green, 0)
    grecv[row] = gsend[row]

    def spans(i):
        s = lax.div(i, CHUNKS)
        return s, pl.ds(pl.multiple_of(lax.rem(i, CHUNKS) * CHUNK, CHUNK), CHUNK)

    def pick(kind):
        return lambda s, dim, lanes: [
            w_scr[kind, j, 2 * dim + s : 2 * dim + s + 1, lanes] for j in range(6)
        ]

    def dense_x(anchor, rows, xo, s, lanes):
        value, tile = tiles_of(anchor, rows, 8)
        for b, at in ((0, 0), (1, 8), (2, 16), (3, 24), (-1, 32)):
            xo[s, at : at + 8, lanes] = jnp.where(tile == b, value, 0.0)

    def dense_z(anchor, rows, hi_ref, lo_ref, s, lanes):
        value, tile = tiles_of(anchor, rows, 16)
        top, rest = halves(value)
        tile = (tile & 15).astype(F32).astype(BF16)
        none = jnp.zeros_like(top)
        for b in range(16):
            here = tile == jnp.asarray(float(b), BF16)
            hi_ref[s, 16 * b : 16 * b + 16, lanes] = jnp.where(here, top, none)
            lo_ref[s, 16 * b : 16 * b + 16, lanes] = jnp.where(here, rest, none)

    def dense_all(i, s, kind, xo, yo, hi_ref, lo_ref):
        rows_of = pick(kind)
        for k in range(CHUNK // 128):
            lanes = pl.ds(pl.multiple_of(i * CHUNK + 128 * k, 128), 128)
            dense_x(cell[0, s : s + 1, lanes] - row * 32, rows_of(s, 0, lanes), xo, s, lanes)
            anchor = cell[1, s : s + 1, lanes] - col * 16
            value, tile = tiles_of(anchor, rows_of(s, 1, lanes), 8)
            for b, at in ((0, 0), (1, 8), (-1, 16)):
                y = jnp.where(tile == b, value, 0.0)
                yo[s, at : at + 8, lanes] = y
                if kind == 0:
                    yq_scr[s, at : at + 8, lanes] = y * yq_scr[s, 24:25, lanes]
            dense_z(cell[2, s : s + 1, lanes], rows_of(s, 2, lanes), hi_ref, lo_ref, s, lanes)

    def build_next(s):
        def body(i, carry):
            for k in range(CHUNK // 128):
                lanes = pl.ds(pl.multiple_of(i * CHUNK + 128 * k, 128), 128)
                rows_of = [
                    [nw_scr[j, 2 * d + s : 2 * d + s + 1, lanes] for j in range(6)]
                    for d in range(3)
                ]
                dense_x(ncell[0, s : s + 1, lanes] - row * 32, rows_of[0], nx_scr, s, lanes)
                anchor = ncell[1, s : s + 1, lanes] - up_c * 16
                value, tile = tiles_of(anchor, rows_of[1], 8)
                value = jnp.where(tile == -1, value, 0.0) * nq[s : s + 1, lanes]
                nyq_scr[s, :, lanes] = value
                dense_z(ncell[2, s : s + 1, lanes], rows_of[2], nz_hi, nz_lo, s, lanes)
            return carry

        lax.fori_loop(0, CHUNKS, body, 0)

    def build(s):
        def body(i, carry):
            dense_all(i, s, 0, x_scr, y_scr, z_hi, z_lo)
            return carry

        lax.fori_loop(0, CHUNKS, body, 0)

    def build_slopes(i, carry):
        for s in range(2):
            dense_all(i, s, 1, sx_scr, sy_scr, sz_hi, sz_lo)
        return carry

    build(0)

    def put(slot, at, value):
        top, rest = halves(value)
        p_hi[slot, at : at + value.shape[0], :] = top
        p_lo[slot, at : at + value.shape[0], :] = rest

    def pairs(fill, ref, zs, low, high):
        def body(i, carry):
            for slot in range(2):
                fill(slot, *spans(2 * i + slot))
            for slot in range(2):
                s, lanes = spans(2 * i + slot)
                a = p_hi[slot, low:high, :], p_lo[slot, low:high, :]
                b = zs[0][s, :, lanes], zs[1][s, :, lanes]
                ref[s, low:high, :] += triple_nt(a, b)
            return carry

        return body

    def fill_next(slot, s, lanes):
        for k in range(5):
            put(slot, 32 * k, nx_scr[s, 0:32, lanes] * nyq_scr[s, 3 + k : 4 + k, lanes])
        edge = nyq_scr[s, :, lanes]
        for k in range(3):
            first = edge * nx_scr[s, 35 + 2 * k : 36 + 2 * k, lanes]
            if k < 2:
                second = edge * nx_scr[s, 36 + 2 * k : 37 + 2 * k, lanes]
            else:
                second = jnp.zeros_like(first)
            put(slot, YH + 16 * k, jnp.concatenate([first, second], axis=0))

    def fill_inner(slot, s, lanes):
        for x in range(32):
            put(slot, 16 * x, yq_scr[s, 0:16, lanes] * x_scr[s, x : x + 1, lanes])

    def fill_edge(slot, s, lanes):
        for k in range(5):
            put(slot, 512 + 16 * k, yq_scr[s, 0:16, lanes] * x_scr[s, 35 + k : 36 + k, lanes])

    def fill_both(slot, s, lanes):
        fill_inner(slot, s, lanes)
        fill_edge(slot, s, lanes)

    nacc[...] = jnp.zeros_like(nacc)
    mesh[...] = jnp.zeros_like(mesh)
    edges = []

    def half(s):
        return s * CHUNKS // 2, (s + 1) * CHUNKS // 2

    def spread_own(s, fill, low, high):
        lax.fori_loop(*half(s), pairs(fill, mesh, (z_hi, z_lo), low, high), 0)

    def spread_next(s):
        lax.fori_loop(*half(s), pairs(fill_next, nacc, (nz_hi, nz_lo), 0, YH + CH), 0)

    def send_edge(s):
        view = mesh.at[s].reshape(MESH_ROWS // 16, 16, 256)
        for k in range(5):
            view[32 + k, 8:16] += nacc[s, YH + 8 * k : YH + 8 * k + 8]
        edges.append(remote(mesh.at[s, 512:MESH_ROWS], xr.at[s], 8 + 2 * s, 9 + 2 * s, (dn_r, col)))
        edges[s].start()

    spread_own(0, fill_both, 0, MESH_ROWS)
    for copy in atoms:
        copy.wait()
    values, _ = spline_values(jnp.concatenate([nfrac[0], nfrac[1], nfrac[2]], axis=0))
    for j in range(6):
        nw_scr[j] = values[j]
    build_next(0)
    spread_next(0)
    send_edge(0)

    pl.semaphore_wait(gate, ROWS - 1)
    first = me == 0

    @pl.when(col == COLS // 2)
    def _():
        gone[...] = infl[:, 0, :]
        remote(gone, glast.at[row], 12, 13, (0, 0)).start()

    build(1)
    build_next(1)
    spread_own(1, fill_edge, 512, MESH_ROWS)
    spread_next(1)
    send_edge(1)

    class Exchange:
        def __init__(self, src, dst, par, first):
            self.src, self.dst, self.first = src.at[par], dst.at[par], first

        def start(self):
            for offset in OFFSETS:
                to = device(*offset)
                src = self.src.at[to[0] * COLS + to[1]]
                remote(src, self.dst.at[me], self.first, self.first + 1, to).start()
            self.dst[me] = self.src[me]

        def wait(self):
            every = slice(0, DEVS - 1)
            remote(
                self.src.at[every], self.dst.at[every], self.first, self.first + 1, (up_r, col)
            ).wait()

    forward = [Exchange(sbuf, rbuf, s, 14 + 2 * s) for s in range(2)]
    backward = [Exchange(tbuf, qbuf, s, 18 + 2 * s) for s in range(2)]

    def send_forward(s):
        edges[s].wait()
        view = mesh.at[s].reshape(MESH_ROWS // 16, 16, 256)
        for k in range(5):
            view[0:32, 11 + k, :] += nacc[s, 32 * k : 32 * k + 32]
        for k in range(5):
            view[27 + k] += xr[s, 16 * k : 16 * k + 16]
        a = triple_nt((tab[0], tab[1]), halves(mesh[s, 0:512]))
        for reim in range(2):
            for q in range(4):
                sbuf[s, :, 4 * reim + q, :] = a[
                    128 * reim : 128 * reim + 128, 128 * q : 128 * q + 128
                ]
        forward[s].start()

    for copy in loads[1:]:
        copy.wait()

    send_forward(0)
    spread_own(1, fill_inner, 0, 512)

    for h in range(2):
        fc, fs, lc, ls = [tab[2 + 2 * k + h] for k in range(4)]
        for ref, c, q in ((fb, fc, fs), (gb, fc, -fs), (lb, lc, -ls)):
            ref[h, 0:256, 0:256] = c
            ref[h, 0:256, 256:512] = q
            ref[h, 256:512, 0:256] = -q
            ref[h, 256:512, 256:512] = c
    some = slice(0, ROWS - 1)
    remote(gsend.at[some], grecv.at[some], 0, 1, (up_r, col)).wait()
    lane = lax.broadcasted_iota(jnp.int32, (16, 256), 1)

    def trade(bits, load, store):
        for rest in range(4):
            base = [(a << bits[0]) + (b << bits[1]) + (rest << (2 if bits[0] == 0 else 0))
                    for b in range(2) for a in range(2)]
            blocks = [load(k) for k in base]
            for i, bit in enumerate(bits):
                step = 1 << bit
                low = (lane & step) == 0
                for k in range(4):
                    if k & (1 << i):
                        continue
                    a, b = blocks[k], blocks[k | (1 << i)]
                    blocks[k] = jnp.where(low, a, pltpu.roll(b, step, 1))
                    blocks[k | (1 << i)] = jnp.where(low, pltpu.roll(a, 256 - step, 1), b)
            for k, block in zip(base, blocks):
                store(k, block)

    def in_mode_order(ref, plane, scale):
        def load(k):
            return ref[k // 2, 16 * (k % 2) : 16 * (k % 2) + 16, :] * scale

        def keep(k, block):
            swap[16 * k : 16 * k + 16, :] = block

        def put_in_place(k, block):
            at = 128 * (k % 2) + 16 * (k // 2)
            green[plane, at : at + 16, :] = block

        trade((0, 1), load, keep)
        trade((2, 3), lambda k: swap[16 * k : 16 * k + 16, :], put_in_place)

    unit = 1.0 / float(K) ** 3
    lax.fori_loop(0, CHUNKS, build_slopes, 0)
    in_mode_order(grecv, 0, jnp.where(first, unit, 2.0 * unit))

    @pl.when(first)
    def _():
        remote(glast, glast, 12, 13, (1, 0)).wait_recv()
        in_mode_order(glast, 1, unit)

    @pl.when(col == COLS // 2)
    def _():
        remote(gone, glast.at[0], 12, 13, (0, 0)).wait_send()

    send_forward(1)

    tc, ts = twid[0], twid[1]

    def stacked(buf, par):
        parts = [
            jnp.concatenate([buf[par, :, 2 * j, :], buf[par, :, 2 * j + 1, :]], axis=1)
            for j in range(4)
        ]
        return jnp.concatenate(parts, axis=0)

    def modes(u):
        ur, ui = u[0:256], u[256:512]
        v = jnp.concatenate([ur * tc + ui * ts, ui * tc - ur * ts], axis=1)
        return triple_nn(halves(v), (lb[0], lb[1]))

    def turn(s, carry):
        Exchange(sbuf, rbuf, s, 14 + 2 * s).wait()

        @pl.when(me != 0)
        def _():
            u = triple_nn((fb[0], fb[1]), halves(stacked(rbuf, s)))
            escr[...] = jnp.concatenate([green[0], green[0]], axis=1) * modes(u)

        @pl.when(me == 0)
        def _():
            x = halves(stacked(rbuf, s))
            left = fb[0, :, 0:256], fb[1, :, 0:256]
            a = modes(triple_nn(left, (x[0][0:256], x[1][0:256])))
            b = modes(triple_nn(left, (x[0][256:512], x[1][256:512])))
            escr[:, 0:256] = green[0] * a[:, 0:256] - green[1] * b[:, 256:512]
            escr[:, 256:512] = green[0] * a[:, 256:512] + green[1] * b[:, 0:256]

        b = triple_nt(halves(escr[...]), (lb[0], lb[1]))
        br, bi = b[:, 0:256], b[:, 256:512]
        h = jnp.concatenate([br * tc - bi * ts, bi * tc + br * ts], axis=0)
        t = triple_nn((gb[0], gb[1]), halves(h))
        for j in range(4):
            for lh in range(2):
                tbuf[s, :, 2 * j + lh, :] = t[
                    128 * j : 128 * j + 128, 128 * lh : 128 * lh + 128
                ]
        Exchange(tbuf, qbuf, s, 18 + 2 * s).start()
        return carry

    lax.fori_loop(0, 2, turn, 0)

    back = []

    def take_back(s):
        backward[s].wait()
        q = stacked(qbuf, s)
        for xh in range(2):
            picked = jnp.concatenate(
                [q[128 * xh : 128 * xh + 128], q[256 + 128 * xh : 384 + 128 * xh]], axis=0
            )
            pot[s, 256 * xh : 256 * xh + 256, :] = triple_nn(halves(picked.T), (tab[0], tab[1]))
        view = pot.at[s].reshape(32, 16, 256)
        for k in range(5):
            ys[s, 32 * k : 32 * k + 32] = view[:, 11 + k, :]
        for k in range(5):
            corner[s, 8 * k : 8 * k + 8] = view[27 + k, 8:16]
        at = 22 + 6 * s
        back.append([
            remote(ys.at[s], yb.at[s], at, at + 1, (row, up_c)),
            remote(pot.at[s, 432:512], xb.at[s], at + 2, at + 3, (up_r, col)),
            remote(corner.at[s], cb.at[s], at + 4, at + 5, (up_r, up_c)),
        ])
        for copy in back[s]:
            copy.start()
        spread_out(fint, s, 0, pot[s])

    def take_halo(s):
        for copy in back[s]:
            copy.wait()
        for at, ref in ((0, yb), (YH, xb), (YH + XH, cb)):
            spread_out(fhal, s, at, ref[s])

    def spread_out(ref, s, at, value):
        top, rest = halves(value)
        n = value.shape[0]
        ref[s, at : at + n, 0:256] = top
        ref[s, at : at + n, 256:512] = rest
        ref[s, at : at + n, 512:768] = top

    def sample(ref, s, lanes):
        top = jnp.concatenate([z_hi[s, :, lanes], sz_hi[s, :, lanes]], axis=1)
        rest = jnp.concatenate([z_lo[s, :, lanes], sz_lo[s, :, lanes]], axis=1)
        both = dot_nn(ref[s], jnp.concatenate([top, top, rest], axis=0))
        return both[:, 0:GCHUNK], both[:, GCHUNK : 2 * GCHUNK]

    def window(i):
        s = lax.div(i, GCHUNKS)
        return s, pl.ds(pl.multiple_of(lax.rem(i, GCHUNKS) * GCHUNK, GCHUNK), GCHUNK)

    def down(value):
        return jnp.sum(value, axis=0, keepdims=True)

    def twice(body):
        return lambda i, carry: body(2 * i + 1, body(2 * i, carry))

    def gather_inner(i, carry):
        s, lanes = window(i)
        plain, slope = sample(fint, s, lanes)
        a1 = a2 = a3 = jnp.zeros((16, GCHUNK), F32)
        for x in range(32):
            wx, sx = x_scr[s, x : x + 1, lanes], sx_scr[s, x : x + 1, lanes]
            piece = plain[16 * x : 16 * x + 16]
            a1 = a1 + piece * sx
            a2 = a2 + piece * wx
            a3 = a3 + slope[16 * x : 16 * x + 16] * wx
        wy, sy = y_scr[s, 0:16, lanes], sy_scr[s, 0:16, lanes]
        part[s, 0:1, lanes] = down(a1 * wy)
        part[s, 1:2, lanes] = down(a2 * sy)
        part[s, 2:3, lanes] = down(a3 * wy)
        return carry

    def gather_halo(i, carry):
        s, lanes = window(i)
        plain, slope = sample(fhal, s, lanes)
        a1 = a2 = a3 = jnp.zeros((16, GCHUNK), F32)
        b1 = b2 = b3 = jnp.zeros((32, GCHUNK), F32)
        e1 = e2 = e3 = jnp.zeros((8, GCHUNK), F32)
        for k in range(5):
            wy, sy = y_scr[s, 19 + k : 20 + k, lanes], sy_scr[s, 19 + k : 20 + k, lanes]
            wx, sx = x_scr[s, 35 + k : 36 + k, lanes], sx_scr[s, 35 + k : 36 + k, lanes]
            piece = plain[32 * k : 32 * k + 32]
            b1 = b1 + piece * wy
            b2 = b2 + piece * sy
            b3 = b3 + slope[32 * k : 32 * k + 32] * wy
            at = YH + 16 * k
            piece = plain[at : at + 16]
            a1 = a1 + piece * sx
            a2 = a2 + piece * wx
            a3 = a3 + slope[at : at + 16] * wx
            at = YH + XH + 8 * k
            piece = plain[at : at + 8]
            e1 = e1 + piece * sx
            e2 = e2 + piece * wx
            e3 = e3 + slope[at : at + 8] * wx
        wy, sy = y_scr[s, 0:16, lanes], sy_scr[s, 0:16, lanes]
        vy, ty = y_scr[s, 16:24, lanes], sy_scr[s, 16:24, lanes]
        wx, sx = x_scr[s, 0:32, lanes], sx_scr[s, 0:32, lanes]

        def finish(d, a, m, e, n, b, q):
            total = part[s, d : d + 1, lanes] + down(a * m) + down(e * n) + down(b * q)
            forces[d, pl.ds(s, 1), lanes] = -yq_scr[s, 24:25, lanes] * total

        finish(0, a1, wy, e1, vy, b1, sx)
        finish(1, a2, sy, e2, ty, b2, wx)
        finish(2, a3, wy, e3, vy, b3, wx)
        return carry

    def gather(body, s):
        lax.fori_loop(s * GCHUNKS // 2, (s + 1) * GCHUNKS // 2, twice(body), 0)

    take_back(0)
    gather(gather_inner, 0)
    take_back(1)
    gather(gather_inner, 1)
    take_halo(0)
    gather(gather_halo, 0)
    take_halo(1)
    gather(gather_halo, 1)


def shards(consts, cell_index, fraction, charge, atom_count, influence):
    vmem = pl.BlockSpec(memory_space=pltpu.VMEM)
    anywhere = pl.BlockSpec(memory_space=pl.ANY)
    args = [
        jnp.transpose(cell_index, (1, 0, 2)), jnp.transpose(fraction, (1, 0, 2)), charge,
        jnp.transpose(atom_count), influence, jnp.asarray(consts[0]), jnp.asarray(consts[1]),
    ]
    v = pltpu.VMEM
    scratch = [
        v((32, 16, 256), F32), v((10, 256, 256), BF16), v((2, 256, 256), F32),
        v((2, 6, 6, ATOMS), F32), v((2, 40, ATOMS), F32), v((2, 24, ATOMS), F32),
        v((2, 25, ATOMS), F32), v((2, 256, ATOMS), BF16), v((2, 256, ATOMS), BF16),
        v((2, 40, ATOMS), F32), v((2, 24, ATOMS), F32), v((2, 256, ATOMS), BF16),
        v((2, 256, ATOMS), BF16), v((2, MESH_ROWS, CHUNK), BF16), v((2, MESH_ROWS, CHUNK), BF16),
        v((3, 2, ATOMS), jnp.int32), v((3, 2, ATOMS), F32), v((2, ATOMS), F32), v((2, ATOMS), F32),
        v((6, 6, ATOMS), F32), v((2, 40, ATOMS), F32), v((2, 8, ATOMS), F32),
        v((2, 256, ATOMS), BF16), v((2, 256, ATOMS), BF16),
        v((2, YH + CH, 256), F32), v((2, XH, 256), F32), v((2, MESH_ROWS, 256), F32),
        v((ROWS, 32, 256), F32), v((ROWS, 32, 256), F32), v((ROWS, 32, 256), F32),
        v((2, 256, 256), F32), v((2, 512, 512), BF16), v((2, 512, 512), BF16),
        v((2, 512, 512), BF16), v((256, 512), F32),
        v((2, DEVS, 8, 128), F32), v((2, DEVS, 8, 128), F32), v((2, DEVS, 8, 128), F32),
        v((2, DEVS, 8, 128), F32), v((2, 512, 256), F32),
        v((2, YH, 256), F32), v((2, 40, 256), F32),
        v((2, YH, 256), F32), v((2, XH, 256), F32), v((2, 40, 256), F32),
        v((2, 512, 768), BF16), v((2, HALO, 768), BF16), v((2, 3, ATOMS), F32),
        v((256, 256), F32), v((32, 256), F32),
        pltpu.SemaphoreType.DMA((34,)), pltpu.SemaphoreType.DMA((3,)), pltpu.SemaphoreType.REGULAR,
    ]
    out = pl.pallas_call(
        kernel,
        out_shape=jax.ShapeDtypeStruct((3, 2, ATOMS), F32),
        in_specs=[vmem] * 4 + [anywhere] * 3,
        out_specs=vmem,
        scratch_shapes=scratch,
        compiler_params=pltpu.CompilerParams(
            collective_id=0, has_side_effects=True, vmem_limit_bytes=66_000_000
        ),
    )(*args)
    return jnp.transpose(out, (1, 0, 2))


def solution(mesh):
    placed = (
        P(None, None, ("row", "col")),
        P(None, None, ("row", "col")),
        P(None, ("row", "col")),
        P(None, ("row", "col")),
        P("row", "col", None),
    )
    return jax.shard_map(
        functools.partial(shards, tables()), mesh=mesh, in_specs=placed,
        out_specs=P(None, None, ("row", "col")), check_vma=False,
    )
```

time: 78.9 us -> 64.6 us (0.82)
  Pallas kernels: 77.2 us -> 62.9 us
    pallas_call x1, Pallas kernels: 77.2 us -> 62.9 us  [shards(): pl.pallas_call(kernel, out_shape=jax.ShapeDtypeStruct((3, 2, ATOMS), F32)...]
where the time goes in v2:
time: 64.6 us; the launch traced here: 64.4 us
  Pallas kernels  62.9 us (97%)
  local copies, waits for them, and re-layouts  1.42 us (2%)
    pallas_call x1, Pallas kernels, shards(): pl.pallas_call(kernel, out_shape=jax.ShapeDtypeStruct((3, 2, ATOMS), F32)...  62.9 us
    unnamed x1, local copies, waits for them, and re-layouts  1.42 us

profile of v2, /device:TPU:1, one launch (start us, length us, event | category | flops | bytes accessed | tf_op | source)
XLA Modules:
  0.0 64.4 jit_solution(9863847743920921166)
XLA Ops:
  0.0 62.9 %shard_map.73 = f32[3,2,2048]{2,1,0:T(2,128)} custom-call(s32[3,2,2048]{2,1,0:T(2,128)} %bitcast.5, f32[3,2,2048]{2,1,0:T(2,128)} %bitcast.6, f32[2,2048]{1,0:T(2,128)} %charge.1, s32[1,2]{1,0:T(1,128)} %bitcast.7, f32[32,16,256]{2,1,0:T(8,128)} %infl_hbm.1, bf16[10,256,256]{2,1,0:T(8,128)(2,1)} %constant.4.clone.tab_hbm, f32[2,256,256]{2,1,0:T(8,128)} %constant.5.clone.twid_hbm), custom_call_target="tpu_custom_call" | custom-call | tf_op jit(solution)/shard_map/pallas_call | solution.py:662
  62.9 1.4 %copy.9 = f32[2,3,2048]{2,0,1:T(2,128)} copy(f32[2,3,2048]{2,0,1:T(2,128)} %bitcast.4) | data formatting | bytes 98304

commit v3 on v2

--- a/solution.py
+++ b/solution.py
@@ -122,9 +122,9 @@
 
 
 def kernel(
-    cell, frac, charge, count, infl_hbm, tab_hbm, twid_hbm,
+    cell_hbm, frac_hbm, charge_hbm, count_hbm, infl_hbm, tab_hbm, twid_hbm,
     forces,
-    infl, tab, twid, w_scr, x_scr, y_scr, yq_scr, z_hi, z_lo, sx_scr, sy_scr, sz_hi, sz_lo,
+    cell, frac, charge, count, infl, tab, twid, w_scr, x_scr, y_scr, yq_scr, z_hi, z_lo, sx_scr, sy_scr, sz_hi, sz_lo,
     p_hi, p_lo, ncell, nfrac, qs, nq, nw_scr, nx_scr, nyq_scr, nz_hi, nz_lo, nacc, xr, mesh, gsend, grecv, glast, green, fb, gb, lb, escr,
     sbuf, rbuf, tbuf, qbuf, pot, ys, corner, yb, xb, cb, fint, fhal, part, swap, gone,
     sems, local, gate,
@@ -152,7 +152,13 @@
         pltpu.make_async_copy(tab_hbm, tab, local.at[1]),
         pltpu.make_async_copy(twid_hbm, twid, local.at[2]),
     ]
-    for copy in loads:
+    inputs = [
+        pltpu.make_async_copy(src, dst, local.at[3 + k])
+        for k, (src, dst) in enumerate((
+            (cell_hbm, cell), (frac_hbm, frac), (charge_hbm, charge), (count_hbm, count)
+        ))
+    ]
+    for copy in inputs + loads:
         copy.start()
 
     barrier = pltpu.get_barrier_semaphore()
@@ -181,6 +187,8 @@
             device_id=to, device_id_type=MESH,
         )
 
+    for copy in inputs:
+        copy.wait()
     slot = lax.broadcasted_iota(jnp.int32, (1, ATOMS), 1)
     values, slopes = spline_values(jnp.concatenate([frac[0], frac[1], frac[2]], axis=0))
     for j in range(6):
@@ -192,9 +200,13 @@
         qs[s : s + 1] = masked
 
     loads[0].wait()
-    late = jnp.full((32, 256), col >= COLS // 2)
-    for k in range(ROWS):
-        gsend[k] = jnp.where(late, infl[:, 2 * k + 1, :], infl[:, 2 * k, :])
+    for odd in range(2):
+
+        @pl.when(lax.div(col, COLS // 2) == odd)
+        def _():
+            for k in range(ROWS):
+                gsend[k] = infl[:, 2 * k + odd, :]
+
     pl.semaphore_wait(barrier, ROWS + COLS - 2)
     lax.fori_loop(1, ROWS, vouch, 0)
     atoms = [
@@ -562,8 +574,13 @@
     def down(value):
         return jnp.sum(value, axis=0, keepdims=True)
 
-    def twice(body):
-        return lambda i, carry: body(2 * i + 1, body(2 * i, carry))
+    def four(body):
+        def several(i, carry):
+            for k in range(4):
+                carry = body(4 * i + k, carry)
+            return carry
+
+        return several
 
     def gather_inner(i, carry):
         s, lanes = window(i)
@@ -618,7 +635,7 @@
         return carry
 
     def gather(body, s):
-        lax.fori_loop(s * GCHUNKS // 2, (s + 1) * GCHUNKS // 2, twice(body), 0)
+        lax.fori_loop(s * GCHUNKS // 4, (s + 1) * GCHUNKS // 4, four(body), 0)
 
     take_back(0)
     gather(gather_inner, 0)
@@ -639,7 +656,8 @@
     ]
     v = pltpu.VMEM
     scratch = [
-        v((32, 16, 256), F32), v((10, 256, 256), BF16), v((2, 256, 256), F32),
+        v((3, 2, ATOMS), jnp.int32), v((3, 2, ATOMS), F32), v((2, ATOMS), F32),
+        v((1, 2), jnp.int32), v((32, 16, 256), F32), v((10, 256, 256), BF16), v((2, 256, 256), F32),
         v((2, 6, 6, ATOMS), F32), v((2, 40, ATOMS), F32), v((2, 24, ATOMS), F32),
         v((2, 25, ATOMS), F32), v((2, 256, ATOMS), BF16), v((2, 256, ATOMS), BF16),
         v((2, 40, ATOMS), F32), v((2, 24, ATOMS), F32), v((2, 256, ATOMS), BF16),
@@ -657,12 +675,12 @@
         v((2, YH, 256), F32), v((2, XH, 256), F32), v((2, 40, 256), F32),
         v((2, 512, 768), BF16), v((2, HALO, 768), BF16), v((2, 3, ATOMS), F32),
         v((256, 256), F32), v((32, 256), F32),
-        pltpu.SemaphoreType.DMA((34,)), pltpu.SemaphoreType.DMA((3,)), pltpu.SemaphoreType.REGULAR,
+        pltpu.SemaphoreType.DMA((34,)), pltpu.SemaphoreType.DMA((7,)), pltpu.SemaphoreType.REGULAR,
     ]
     out = pl.pallas_call(
         kernel,
-        out_shape=jax.ShapeDtypeStruct((3, 2, ATOMS), F32),
-        in_specs=[vmem] * 4 + [anywhere] * 3,
+        out_shape=pltpu.VMEM((3, 2, ATOMS), F32),
+        in_specs=[anywhere] * 7,
         out_specs=vmem,
         scratch_shapes=scratch,
         compiler_params=pltpu.CompilerParams(

time: 64.6 us -> 61.7 us (0.955)
  Pallas kernels: 62.9 us -> 61 us
  local copies, waits for them, and re-layouts: 1.42 us -> 0.62 us
    pallas_call x1, Pallas kernels: 62.9 us -> 61 us  [shards(): pl.pallas_call(kernel, out_shape=pltpu.VMEM((3, 2, ATOMS), F32), in_specs...]
    unnamed x1, local copies, waits for them, and re-layouts: 1.42 us -> 0.62 us
where the time goes in v3:
time: 61.7 us; the launch traced here: 61.6 us
  Pallas kernels  61 us (99%)
  local copies, waits for them, and re-layouts  0.62 us (1%)
    pallas_call x1, Pallas kernels, shards(): pl.pallas_call(kernel, out_shape=pltpu.VMEM((3, 2, ATOMS), F32), in_specs...  61 us

profile of v3, /device:TPU:1, one launch (start us, length us, event | category | flops | bytes accessed | tf_op | source)
XLA Modules:
  0.0 61.6 jit_solution(10497947523410426169)
XLA Ops:
  0.0 61.0 %shard_map.73 = f32[3,2,2048]{2,1,0:T(2,128)S(1)} custom-call(s32[3,2,2048]{2,1,0:T(2,128)} %bitcast.5, f32[3,2,2048]{2,1,0:T(2,128)} %bitcast.6, f32[2,2048]{1,0:T(2,128)} %charge_hbm.1, s32[1,2]{1,0:T(1,128)} %bitcast.7, f32[32,16,256]{2,1,0:T(8,128)} %infl_hbm.1, bf16[10,256,256]{2,1,0:T(8,128)(2,1)} %constant.4.clone.tab_hbm, ...), custom_call_target="tpu_custom_call" | custom-call | tf_op jit(solution)/shard_map/pallas_call | solution.py:680
  61.0 0.6 %copy.9 = f32[2,3,2048]{2,0,1:T(2,128)} copy(f32[2,3,2048]{2,0,1:T(2,128)S(1)} %bitcast.4) | data formatting | bytes 98304

commit v4 on v3

--- a/solution.py
+++ b/solution.py
@@ -104,6 +104,17 @@
     return dot_nn(left, jnp.concatenate([b[0], b[0], b[1]], axis=0))
 
 
+def three_nn(a, b):
+    return dot_nn(a[0], b[0]) + dot_nn(a[1], b[0]) + dot_nn(a[0], b[1])
+
+
+def tall_nn(a, b):
+    n = a[0].shape[0] // 2
+    return jnp.concatenate(
+        [three_nn((a[0][q], a[1][q]), b) for q in (slice(0, n), slice(n, 2 * n))], axis=0
+    )
+
+
 def triple_nt(a, b):
     left = jnp.concatenate([a[0], a[1], a[0]], axis=1)
     return dot_nt(left, jnp.concatenate([b[0], b[0], b[1]], axis=1))
@@ -490,29 +501,29 @@
     def modes(u):
         ur, ui = u[0:256], u[256:512]
         v = jnp.concatenate([ur * tc + ui * ts, ui * tc - ur * ts], axis=1)
-        return triple_nn(halves(v), (lb[0], lb[1]))
+        return three_nn(halves(v), (lb[0], lb[1]))
 
     def turn(s, carry):
         Exchange(sbuf, rbuf, s, 14 + 2 * s).wait()
 
         @pl.when(me != 0)
         def _():
-            u = triple_nn((fb[0], fb[1]), halves(stacked(rbuf, s)))
+            u = tall_nn((fb[0], fb[1]), halves(stacked(rbuf, s)))
             escr[...] = jnp.concatenate([green[0], green[0]], axis=1) * modes(u)
 
         @pl.when(me == 0)
         def _():
             x = halves(stacked(rbuf, s))
             left = fb[0, :, 0:256], fb[1, :, 0:256]
-            a = modes(triple_nn(left, (x[0][0:256], x[1][0:256])))
-            b = modes(triple_nn(left, (x[0][256:512], x[1][256:512])))
+            a = modes(tall_nn(left, (x[0][0:256], x[1][0:256])))
+            b = modes(tall_nn(left, (x[0][256:512], x[1][256:512])))
             escr[:, 0:256] = green[0] * a[:, 0:256] - green[1] * b[:, 256:512]
             escr[:, 256:512] = green[0] * a[:, 256:512] + green[1] * b[:, 0:256]
 
         b = triple_nt(halves(escr[...]), (lb[0], lb[1]))
         br, bi = b[:, 0:256], b[:, 256:512]
         h = jnp.concatenate([br * tc - bi * ts, bi * tc + br * ts], axis=0)
-        t = triple_nn((gb[0], gb[1]), halves(h))
+        t = tall_nn((gb[0], gb[1]), halves(h))
         for j in range(4):
             for lh in range(2):
                 tbuf[s, :, 2 * j + lh, :] = t[

time: 61.7 us -> 60.5 us (0.981)
  Pallas kernels: 61 us -> 59.7 us
    pallas_call x1, Pallas kernels: 61 us -> 59.7 us  [shards(): pl.pallas_call(kernel, out_shape=pltpu.VMEM((3, 2, ATOMS), F32), in_specs...]
where the time goes in v4:
time: 60.5 us; the launch traced here: 60.3 us
  Pallas kernels  59.7 us (99%)
  local copies, waits for them, and re-layouts  0.62 us (1%)
    pallas_call x1, Pallas kernels, shards(): pl.pallas_call(kernel, out_shape=pltpu.VMEM((3, 2, ATOMS), F32), in_specs...  59.7 us

profile of v4, /device:TPU:1, one launch (start us, length us, event | category | flops | bytes accessed | tf_op | source)
XLA Modules:
  0.0 60.3 jit_solution(16249056840114544385)
XLA Ops:
  0.0 59.7 %shard_map.73 = f32[3,2,2048]{2,1,0:T(2,128)S(1)} custom-call(s32[3,2,2048]{2,1,0:T(2,128)} %bitcast.5, f32[3,2,2048]{2,1,0:T(2,128)} %bitcast.6, f32[2,2048]{1,0:T(2,128)} %charge_hbm.1, s32[1,2]{1,0:T(1,128)} %bitcast.7, f32[32,16,256]{2,1,0:T(8,128)} %infl_hbm.1, bf16[10,256,256]{2,1,0:T(8,128)(2,1)} %constant.4.clone.tab_hbm, ...), custom_call_target="tpu_custom_call" | custom-call | tf_op jit(solution)/shard_map/pallas_call | solution.py:691
  59.7 0.6 %copy.9 = f32[2,3,2048]{2,0,1:T(2,128)} copy(f32[2,3,2048]{2,0,1:T(2,128)S(1)} %bitcast.4) | data formatting | bytes 98304

commit v5 on v4

--- a/solution.py
+++ b/solution.py
@@ -368,6 +368,7 @@
         edges[s].start()
 
     spread_own(0, fill_both, 0, MESH_ROWS)
+    build(1)
     for copy in atoms:
         copy.wait()
     values, _ = spline_values(jnp.concatenate([nfrac[0], nfrac[1], nfrac[2]], axis=0))
@@ -385,7 +386,6 @@
         gone[...] = infl[:, 0, :]
         remote(gone, glast.at[row], 12, 13, (0, 0)).start()
 
-    build(1)
     build_next(1)
     spread_own(1, fill_edge, 512, MESH_ROWS)
     spread_next(1)

time: 60.5 us -> 58.9 us (0.974)
  Pallas kernels: 59.7 us -> 58.1 us
    pallas_call x1, Pallas kernels: 59.7 us -> 58.1 us  [shards(): pl.pallas_call(kernel, out_shape=pltpu.VMEM((3, 2, ATOMS), F32), in_specs...]
where the time goes in v5:
time: 58.9 us; the launch traced here: 58.8 us
  Pallas kernels  58.1 us (99%)
  local copies, waits for them, and re-layouts  0.62 us (1%)
    pallas_call x1, Pallas kernels, shards(): pl.pallas_call(kernel, out_shape=pltpu.VMEM((3, 2, ATOMS), F32), in_specs...  58.1 us

profile of v5, /device:TPU:1, one launch (start us, length us, event | category | flops | bytes accessed | tf_op | source)
XLA Modules:
  0.0 58.8 jit_solution(14794114218556363335)
XLA Ops:
  0.0 58.1 %shard_map.73 = f32[3,2,2048]{2,1,0:T(2,128)S(1)} custom-call(s32[3,2,2048]{2,1,0:T(2,128)} %bitcast.5, f32[3,2,2048]{2,1,0:T(2,128)} %bitcast.6, f32[2,2048]{1,0:T(2,128)} %charge_hbm.1, s32[1,2]{1,0:T(1,128)} %bitcast.7, f32[32,16,256]{2,1,0:T(8,128)} %infl_hbm.1, bf16[10,256,256]{2,1,0:T(8,128)(2,1)} %constant.4.clone.tab_hbm, ...), custom_call_target="tpu_custom_call" | custom-call | tf_op jit(solution)/shard_map/pallas_call | solution.py:691
  58.1 0.6 %copy.9 = f32[2,3,2048]{2,0,1:T(2,128)} copy(f32[2,3,2048]{2,0,1:T(2,128)S(1)} %bitcast.4) | data formatting | bytes 98304

commit v6 on v5

--- a/solution.py
+++ b/solution.py
@@ -201,22 +201,10 @@
     for copy in inputs:
         copy.wait()
     slot = lax.broadcasted_iota(jnp.int32, (1, ATOMS), 1)
-    values, slopes = spline_values(jnp.concatenate([frac[0], frac[1], frac[2]], axis=0))
-    for j in range(6):
-        w_scr[0, j] = values[j]
-        w_scr[1, j] = slopes[j]
     for s in range(2):
         masked = jnp.where(slot < count[0:1, s : s + 1], charge[s : s + 1], 0.0)
         yq_scr[s, 24:25] = masked
         qs[s : s + 1] = masked
-
-    loads[0].wait()
-    for odd in range(2):
-
-        @pl.when(lax.div(col, COLS // 2) == odd)
-        def _():
-            for k in range(ROWS):
-                gsend[k] = infl[:, 2 * k + odd, :]
 
     pl.semaphore_wait(barrier, ROWS + COLS - 2)
     lax.fori_loop(1, ROWS, vouch, 0)
@@ -227,6 +215,14 @@
     for copy in atoms:
         copy.start()
 
+    loads[0].wait()
+    for odd in range(2):
+
+        @pl.when(lax.div(col, COLS // 2) == odd)
+        def _():
+            for k in range(ROWS):
+                gsend[k] = infl[:, 2 * k + odd, :]
+
     def send_green(k, carry):
         there = lax.rem(row + k, ROWS)
         remote(gsend.at[there], grecv.at[row], 0, 1, (there, col)).start()
@@ -234,6 +230,11 @@
 
     lax.fori_loop(1, ROWS, send_green, 0)
     grecv[row] = gsend[row]
+
+    values, slopes = spline_values(jnp.concatenate([frac[0], frac[1], frac[2]], axis=0))
+    for j in range(6):
+        w_scr[0, j] = values[j]
+        w_scr[1, j] = slopes[j]
 
     def spans(i):
         s = lax.div(i, CHUNKS)

time: 58.9 us -> 59.4 us (level)
  Pallas kernels: 58.1 us -> 58.7 us
where the time goes in v6:
time: 59.4 us; the launch traced here: 59.3 us
  Pallas kernels  58.7 us (99%)
  local copies, waits for them, and re-layouts  0.62 us (1%)
    pallas_call x1, Pallas kernels, shards(): pl.pallas_call(kernel, out_shape=pltpu.VMEM((3, 2, ATOMS), F32), in_specs...  58.7 us

profile of v6, /device:TPU:1, one launch (start us, length us, event | category | flops | bytes accessed | tf_op | source)
XLA Modules:
  0.0 59.3 jit_solution(13646678620532246557)
XLA Ops:
  0.0 58.7 %shard_map.73 = f32[3,2,2048]{2,1,0:T(2,128)S(1)} custom-call(s32[3,2,2048]{2,1,0:T(2,128)} %bitcast.5, f32[3,2,2048]{2,1,0:T(2,128)} %bitcast.6, f32[2,2048]{1,0:T(2,128)} %charge_hbm.1, s32[1,2]{1,0:T(1,128)} %bitcast.7, f32[32,16,256]{2,1,0:T(8,128)} %infl_hbm.1, bf16[10,256,256]{2,1,0:T(8,128)(2,1)} %constant.4.clone.tab_hbm, ...), custom_call_target="tpu_custom_call" | custom-call | tf_op jit(solution)/shard_map/pallas_call | solution.py:692
  58.7 0.6 %copy.9 = f32[2,3,2048]{2,0,1:T(2,128)} copy(f32[2,3,2048]{2,0,1:T(2,128)S(1)} %bitcast.4) | data formatting | bytes 98304
